TPU v7x, 256 devices: a whole 4x4x8 slice. The times are simulated.
256 devices in a mesh: section: 8 (over z_hi, x), dp: 32 (over y, z_lo, core).
Axes of the slice: x: 4, y: 4, z: 8 (z_hi: 2, z_lo: 4; z = z_hi * 4 + z_lo), core: 2. Of those that a mesh axis runs over, the one named last changes fastest.
Arguments:
- inputs: bfloat16 [4, 4096, 1536], P(None, 'dp'), may hold values from -6 to 6
- out_grad: bfloat16 [4, 4096, 1536], P(None, 'dp'), may hold values from -0.09375 to 0.09375
- guide_bin: int32 [4, 1], replicated, may hold values from 0 to 31
- time_step: int32 [4, 1], replicated, may hold values from 0 to 999
- guide_table: bfloat16 [32, 4608], replicated, may hold values from -3 to 3
- section_table: float32 [8, 3, 1536], P('section'), may hold values from -3 to 3
- value_weight: bfloat16 [8, 1536, 1536], P('section'), may hold values from -0.15625 to 0.15625
- proj_weight: bfloat16 [8, 1536, 1536], P('section'), may hold values from -0.15625 to 0.15625
Outputs:
- value_grad: float32 [8, 1536, 1536], P('section', 'dp')
- proj_grad: float32 [8, 1536, 1536], P('section', 'dp')
- table_grad: float32 [8, 3, 1536], P('section', None, 'dp')
All inputs are finite; a program needn't handle non-finite values.
Results may differ from a plain program's by a relative error of at most 0.017.
Values may be sent and summed in bfloat16 or wider, within the bound.
A program may use at most 128 MiB of HBM per device.

v0:
```python
import math

import jax
import jax.numpy as jnp
from jax import lax
from jax.sharding import Mesh
from jax.sharding import PartitionSpec as P

DP = ("dp_0", "dp_1", "dp_2")


NORM_FLOOR = 0.1


def shifted(value, axis, steps):
    count = lax.axis_size(axis)
    leading, last = (max(0, -steps), min(count, count - steps))
    return lax.ppermute(value, axis, [(source, source + steps) for source in range(leading, last)])


def split_up(value, dim, peers):
    dims = value.shape
    parts = value.reshape(*dims[:dim], peers, dims[dim] // peers, *dims[dim + 1 :])
    return jnp.moveaxis(parts, dim, 0)


def sum_by_chip(value, chips, core, dim):
    sizes = (lax.axis_size(chips), lax.axis_size(core))
    parts = split_up(value, dim, sizes[0] * sizes[1])
    inside = parts.shape[1:]
    parts = parts.reshape(*sizes, *inside).swapaxes(0, 1).reshape(-1, *inside)
    parts = lax.psum_scatter(parts, core, scatter_dimension=0, tiled=True)
    return lax.psum_scatter(parts, chips, scatter_dimension=0, tiled=True)[0]


def summed_on_arrival(value, axis, dim):
    parts = split_up(value, dim, lax.axis_size(axis))
    arrived = lax.all_to_all(parts, axis, split_axis=0, concat_axis=0, tiled=True)
    return arrived.sum(axis=0)


def normalize(hidden):
    centre = jnp.mean(hidden, axis=-1, keepdims=True)
    centred = hidden - centre
    spread = jnp.mean(centred * centred, axis=-1, keepdims=True)
    inverse = lax.rsqrt(spread + NORM_FLOOR)
    return (centred * inverse, inverse)


def conditions(guide_bin, time_step, guide_table):
    total = guide_table.shape[1]
    half = total // 2
    frequency = jnp.exp(-math.log(10000.0) * jnp.arange(half, dtype=jnp.float32) / half)
    angle = time_step.astype(jnp.float32)[..., None] * frequency
    waves = jnp.concatenate([jnp.sin(angle), jnp.cos(angle)], axis=-1)
    bin_count = guide_table.shape[0]
    onehot = (guide_bin[..., None] == jnp.arange(bin_count, dtype=jnp.int32)).astype(jnp.float32)
    picked = jnp.einsum(
        "msb,bw->msw", onehot, guide_table.astype(jnp.float32), precision=lax.Precision.HIGHEST
    )
    return picked + 0.5 * waves


def contract_rows(left, right):
    return lax.dot_general(
        left, right, (((0,), (0,)), ((), ())), preferred_element_type=jnp.float32
    )


def forward_block(block_in, modulation, value_weight, proj_weight):
    width = block_in.shape[1]
    hidden = block_in.astype(jnp.float32)
    normed, inverse = normalize(hidden)
    shift = modulation[:, :width]
    scale = modulation[:, width : 2 * width]
    gate = modulation[:, 2 * width :]
    modulated = (normed * (1.0 + scale) + shift).astype(jnp.bfloat16)
    values = jnp.dot(modulated, value_weight, preferred_element_type=jnp.float32).astype(
        jnp.bfloat16
    )
    projected = jnp.dot(values, proj_weight, preferred_element_type=jnp.float32)
    block_out = (hidden + gate * projected).astype(jnp.bfloat16)
    return (block_out, modulated, values, projected)


def backward_block(block_in, projected, upstream, modulation, value_weight, proj_weight):
    width = block_in.shape[1]
    hidden = block_in.astype(jnp.float32)
    normed, inverse = normalize(hidden)
    scale = modulation[:, width : 2 * width]
    gate = modulation[:, 2 * width :]
    grad_up = upstream.astype(jnp.float32)
    grad_proj = (gate * grad_up).astype(jnp.bfloat16)
    grad_values = lax.dot_general(
        grad_proj, proj_weight, (((1,), (1,)), ((), ())), preferred_element_type=jnp.float32
    ).astype(jnp.bfloat16)
    grad_mod = lax.dot_general(
        grad_values, value_weight, (((1,), (1,)), ((), ())), preferred_element_type=jnp.float32
    )
    part_table = jnp.stack(
        [
            jnp.sum(grad_mod, axis=0),
            jnp.sum(grad_mod * normed, axis=0),
            jnp.sum(grad_up * projected, axis=0),
        ]
    )
    grad_norm = grad_mod * (1.0 + scale)
    centre_grad = jnp.mean(grad_norm, axis=-1, keepdims=True)
    cross = jnp.mean(grad_norm * normed, axis=-1, keepdims=True)
    grad_in = grad_up + inverse * (grad_norm - centre_grad - normed * cross)
    return (grad_in.astype(jnp.bfloat16), grad_values, grad_proj, part_table)


def per_device(
    inputs, out_grad, guide_bin, time_step, guide_table, section_table, value_weight, proj_weight
):
    sections = lax.axis_size("section")
    section_id = lax.axis_index("section")
    position = lax.axis_index(DP)
    group_size = lax.axis_size(DP)
    tok_dev = inputs.shape[1]
    width = inputs.shape[2]
    value_width = value_weight.shape[2]
    batches = inputs.shape[0]
    samples = guide_bin.shape[1]
    tokens = tok_dev * group_size
    rows_per = tokens // samples
    parts = 1
    unit_rows = tok_dev // parts
    units = batches * parts
    condition = conditions(guide_bin, time_step, guide_table)
    weights_value = value_weight[0]
    weights_proj = proj_weight[0]
    section_row = section_table[0].reshape(-1)
    sample_ids = jnp.arange(samples, dtype=jnp.int32)

    def unit_modulation(unit_id):
        batch_id = unit_id // parts
        piece_id = unit_id % parts
        chosen = lax.dynamic_index_in_dim(condition, batch_id, 0, keepdims=False)
        global_rows = (
            position * tok_dev + piece_id * unit_rows + jnp.arange(unit_rows, dtype=jnp.int32)
        )
        owner = global_rows // rows_per
        onehot = (owner[:, None] == sample_ids[None, :]).astype(jnp.float32)
        picked = jnp.dot(
            onehot, chosen, precision=lax.Precision.HIGHEST, preferred_element_type=jnp.float32
        )
        return picked + section_row

    slots = units + 1
    keep_in = jnp.zeros((slots, unit_rows, width), jnp.bfloat16)
    keep_mod = jnp.zeros((slots, unit_rows, width), jnp.bfloat16)
    keep_val = jnp.zeros((slots, unit_rows, value_width), jnp.bfloat16)
    keep_proj = jnp.zeros((slots, unit_rows, width), jnp.float32)
    arriving = jnp.zeros((unit_rows, width), jnp.bfloat16)

    def forward_tick(carry, tick_id):
        incoming, saved_in, saved_mod, saved_val, saved_proj = carry
        unit_id = tick_id - section_id
        valid = (unit_id >= 0) & (unit_id < units)
        clipped = jnp.clip(unit_id, 0, units - 1)
        first = lax.dynamic_index_in_dim(inputs, clipped, 0, keepdims=False)
        block_in = jnp.where(section_id == 0, first, incoming)

        def forward_active(operand):
            return forward_block(operand, unit_modulation(clipped), weights_value, weights_proj)

        def forward_resting(operand):
            return (
                jnp.zeros_like(operand),
                jnp.zeros_like(operand),
                jnp.zeros((unit_rows, value_width), jnp.bfloat16),
                jnp.zeros((unit_rows, width), jnp.float32),
            )

        block_out, modulated, values, projected = lax.cond(
            valid, forward_active, forward_resting, block_in
        )
        slot_id = jnp.where(valid, unit_id, units)
        saved_in = lax.dynamic_update_index_in_dim(saved_in, block_in, slot_id, 0)
        saved_mod = lax.dynamic_update_index_in_dim(saved_mod, modulated, slot_id, 0)
        saved_val = lax.dynamic_update_index_in_dim(saved_val, values, slot_id, 0)
        saved_proj = lax.dynamic_update_index_in_dim(saved_proj, projected, slot_id, 0)
        sent = shifted(block_out, "section", 1)
        return ((sent, saved_in, saved_mod, saved_val, saved_proj), None)

    ticks = jnp.arange(units + sections - 1, dtype=jnp.int32)
    carry, unused = lax.scan(
        forward_tick, (arriving, keep_in, keep_mod, keep_val, keep_proj), ticks
    )
    arriving, keep_in, keep_mod, keep_val, keep_proj = carry
    store = jnp.zeros((slots, unit_rows, value_width), jnp.bfloat16)
    extra_zero = jnp.zeros((unit_rows, value_width), jnp.bfloat16)
    keep_grad = jnp.zeros((slots, unit_rows, width), jnp.bfloat16)
    proj_sum = jnp.zeros((value_width, width), jnp.float32)
    table_sum = jnp.zeros((3, width), jnp.float32)

    def backward_tick(carry, tick_id):
        incoming, store_now, grads_now, proj_now, table_now = carry
        unit_id = tick_id - (sections - 1 - section_id)
        valid = (unit_id >= 0) & (unit_id < units)
        clipped = jnp.clip(unit_id, 0, units - 1)
        last = lax.dynamic_index_in_dim(out_grad, clipped, 0, keepdims=False)
        upstream = jnp.where(section_id == sections - 1, last, incoming)
        block_in = lax.dynamic_index_in_dim(keep_in, clipped, 0, keepdims=False)
        modulated = lax.dynamic_index_in_dim(keep_mod, clipped, 0, keepdims=False)
        values = lax.dynamic_index_in_dim(keep_val, clipped, 0, keepdims=False)
        projected = lax.dynamic_index_in_dim(keep_proj, clipped, 0, keepdims=False)

        def backward_active(operand):
            grad_in, grad_values, grad_proj, part_table = backward_block(
                block_in, projected, operand, unit_modulation(clipped), weights_value, weights_proj
            )
            part_proj = jnp.zeros((value_width, width), jnp.float32)
            return (grad_in, grad_values, grad_proj, part_proj, part_table)

        def backward_resting(operand):
            return (
                jnp.zeros_like(operand),
                extra_zero,
                jnp.zeros((unit_rows, width), jnp.bfloat16),
                jnp.zeros((value_width, width), jnp.float32),
                jnp.zeros((3, width), jnp.float32),
            )

        grad_in, extra, grad_proj, part_proj, part_table = lax.cond(
            valid, backward_active, backward_resting, upstream
        )
        slot_id = jnp.where(valid, unit_id, units)
        store_now = lax.dynamic_update_index_in_dim(store_now, extra, slot_id, 0)
        grads_now = lax.dynamic_update_index_in_dim(grads_now, grad_proj, slot_id, 0)
        sent = shifted(grad_in, "section", -1)
        return ((sent, store_now, grads_now, proj_now + part_proj, table_now + part_table), None)

    carry, unused = lax.scan(
        backward_tick, (arriving, store, keep_grad, proj_sum, table_sum), ticks
    )
    arriving, store, keep_grad, proj_sum, table_sum = carry
    mod_rows = keep_mod[:units].reshape(units * unit_rows, width)
    grad_rows = store[:units].reshape(units * unit_rows, value_width)
    columns = mod_rows
    value_part = sum_by_chip(contract_rows(columns, grad_rows), ("dp_0", "dp_1"), "dp_2", 0)
    val_rows = keep_val[:units].reshape(units * unit_rows, value_width)
    upper_rows = keep_grad[:units].reshape(units * unit_rows, width)
    columns = val_rows
    proj_part = sum_by_chip(contract_rows(columns, upper_rows), ("dp_0", "dp_1"), "dp_2", 0)
    table_part = summed_on_arrival(table_sum, DP, 1)
    return (value_part[None], proj_part[None], table_part[None])


def solution(mesh):
    finer = Mesh(
        mesh.devices.reshape(mesh.shape["section"], 4, 4, 2), ("section", "dp_0", "dp_1", "dp_2")
    )
    placed = (
        P(None, DP, None),
        P(None, DP, None),
        P(),
        P(),
        P(),
        P("section", None, None),
        P("section", None, None),
        P("section", None, None),
    )
    return jax.shard_map(
        per_device,
        mesh=finer,
        in_specs=placed,
        out_specs=(P("section", DP, None), P("section", DP, None), P("section", None, DP)),
        check_vma=False,
    )
```

profile of v0, /device:TPU:1, one launch (start us, length us, event | category | flops | bytes accessed | tf_op | source)
XLA Modules:
  0.0 849.7 jit_solution(9881502808202706569)
XLA Ops:
  16.7 212.4 %while.38 = (s32[]{:T(128)}, bf16[128,1536]{1,0:T(8,128)(2,1)S(1)}, bf16[5,128,1536]{2,1,0:T(8,128)(2,1)}, bf16[5,128,1536]{2,1,0:T(8,128)(2,1)}, bf16[5,128,153...) while((s32[]{:T(128)}, bf16[128,1536]{1,0:T(8,128)(2,1)S(1)}, ...), condition=%wide.region_5.6_spmd, body=%wide.region_0.5_spmd.sunk | while | flops 1212877184 | bytes 61066352 | solution.py:189
  90.8 11.0 %collective-permute-start = (bf16[128,1536]{1,0:T(8,128)(2,1)S(1)}, bf16[128,1536]{1,0:T(8,128)(2,1)S(1)}, u32[]{:S(2)}, u32[]{:S(2)}) collective-permute-start(bf16[128,1536]{1,0:T(8,128)(2,1)S(1)} %get-tuple-element.936), channel_id=1, source_target_pairs={{0,32},{32,64},{64,96},{96,128},{128,160},{160,192},{192,224},{1,3... | collective-permute-start | bytes 1179656 | tf_op jit(solution)/shard_map/while/body/eval_jaxpr/ppermute | solution.py:18
  167.2 14.9 %collective-permute-start = (bf16[128,1536]{1,0:T(8,128)(2,1)S(1)}, bf16[128,1536]{1,0:T(8,128)(2,1)S(1)}, u32[]{:S(2)}, u32[]{:S(2)}) collective-permute-start(bf16[128,1536]{1,0:T(8,128)(2,1)S(1)} %get-tuple-element.936), channel_id=1, source_target_pairs={{0,32},{32,64},{64,96},{96,128},{128,160},{160,192},{192,224},{1,3... | collective-permute-start | bytes 1179656 | tf_op jit(solution)/shard_map/while/body/eval_jaxpr/ppermute | solution.py:18
  209.5 14.9 %collective-permute-start = (bf16[128,1536]{1,0:T(8,128)(2,1)S(1)}, bf16[128,1536]{1,0:T(8,128)(2,1)S(1)}, u32[]{:S(2)}, u32[]{:S(2)}) collective-permute-start(bf16[128,1536]{1,0:T(8,128)(2,1)S(1)} %get-tuple-element.936), channel_id=1, source_target_pairs={{0,32},{32,64},{64,96},{96,128},{128,160},{160,192},{192,224},{1,3... | collective-permute-start | bytes 1179656 | tf_op jit(solution)/shard_map/while/body/eval_jaxpr/ppermute | solution.py:18
  232.1 256.7 %while.39 = (s32[]{:T(128)}, bf16[128,1536]{1,0:T(8,128)(2,1)S(1)}, bf16[5,128,1536]{2,1,0:T(8,128)(2,1)}, bf16[5,128,1536]{2,1,0:T(8,128)(2,1)}, f32[3,1536]{1,...) while((s32[]{:T(128)}, bf16[128,1536]{1,0:T(8,128)(2,1)S(1)}, ...), condition=%wide.region_16.17_spmd.clone, body=%wide.region_6.16_spmd.clone.sunk | while | flops 1216823168 | bytes 66722920 | solution.py:236
  235.8 12.7 %collective-permute-done.1 = bf16[128,1536]{1,0:T(8,128)(2,1)S(1)} collective-permute-done((bf16[128,1536]{1,0:T(8,128)(2,1)S(1)}, bf16[128,1536]{1,0:T(8,128)(2,1)S(1)}, u32[]{:S(2)}, u32[]{:S(2)}) %collective-permute-start.1) | collective-permute-done | bytes 393248 | tf_op jit(solution)/shard_map/while/body/eval_jaxpr/ppermute | solution.py:18
  252.2 12.8 %collective-permute-done.1 = bf16[128,1536]{1,0:T(8,128)(2,1)S(1)} collective-permute-done((bf16[128,1536]{1,0:T(8,128)(2,1)S(1)}, bf16[128,1536]{1,0:T(8,128)(2,1)S(1)}, u32[]{:S(2)}, u32[]{:S(2)}) %collective-permute-start.1) | collective-permute-done | bytes 393248 | tf_op jit(solution)/shard_map/while/body/eval_jaxpr/ppermute | solution.py:18
  268.7 13.3 %collective-permute-done.1 = bf16[128,1536]{1,0:T(8,128)(2,1)S(1)} collective-permute-done((bf16[128,1536]{1,0:T(8,128)(2,1)S(1)}, bf16[128,1536]{1,0:T(8,128)(2,1)S(1)}, u32[]{:S(2)}, u32[]{:S(2)}) %collective-permute-start.1) | collective-permute-done | bytes 393248 | tf_op jit(solution)/shard_map/while/body/eval_jaxpr/ppermute | solution.py:18
  285.7 14.9 %collective-permute-done.1 = bf16[128,1536]{1,0:T(8,128)(2,1)S(1)} collective-permute-done((bf16[128,1536]{1,0:T(8,128)(2,1)S(1)}, bf16[128,1536]{1,0:T(8,128)(2,1)S(1)}, u32[]{:S(2)}, u32[]{:S(2)}) %collective-permute-start.1) | collective-permute-done | bytes 393248 | tf_op jit(solution)/shard_map/while/body/eval_jaxpr/ppermute | solution.py:18
  304.3 17.7 %collective-permute-done.1 = bf16[128,1536]{1,0:T(8,128)(2,1)S(1)} collective-permute-done((bf16[128,1536]{1,0:T(8,128)(2,1)S(1)}, bf16[128,1536]{1,0:T(8,128)(2,1)S(1)}, u32[]{:S(2)}, u32[]{:S(2)}) %collective-permute-start.1) | collective-permute-done | bytes 393248 | tf_op jit(solution)/shard_map/while/body/eval_jaxpr/ppermute | solution.py:18
  325.6 17.4 %collective-permute-done.1 = bf16[128,1536]{1,0:T(8,128)(2,1)S(1)} collective-permute-done((bf16[128,1536]{1,0:T(8,128)(2,1)S(1)}, bf16[128,1536]{1,0:T(8,128)(2,1)S(1)}, u32[]{:S(2)}, u32[]{:S(2)}) %collective-permute-start.1) | collective-permute-done | bytes 393248 | tf_op jit(solution)/shard_map/while/body/eval_jaxpr/ppermute | solution.py:18
  346.7 41.5 %collective-permute-done.1 = bf16[128,1536]{1,0:T(8,128)(2,1)S(1)} collective-permute-done((bf16[128,1536]{1,0:T(8,128)(2,1)S(1)}, bf16[128,1536]{1,0:T(8,128)(2,1)S(1)}, u32[]{:S(2)}, u32[]{:S(2)}) %collective-permute-start.1) | collective-permute-done | bytes 393248 | tf_op jit(solution)/shard_map/while/body/eval_jaxpr/ppermute | solution.py:18
  389.5 10.8 %conditional.6 = (bf16[128,1536]{1,0:T(8,128)(2,1)S(1)}, f32[3,1536]{1,0:T(4,128)S(1)}, bf16[1,128,1536]{2,1,0:T(8,128)(2,1)S(1)}, bf16[1,128,1536]{2,1,0:T(8,128)(2,1)S(1)}) conditional(s32[]{:T(128)} %convert_element_type.133, () %tuple.119, (pred[]{:T(512)}, s32[]{:T(128)}, bf16[4,128,1536]{2,1,0:T(8,128)(2,1)}, bf16[128,1536]{1,0:T(8,128)(2,1)S(1)}, ...), branch_computations={%region_7.7_spmd, %region_8.15_spmd} | conditional | flops 1216813952 | bytes 63521484 | solution.py:227
  402.6 12.3 %collective-permute-done.1 = bf16[128,1536]{1,0:T(8,128)(2,1)S(1)} collective-permute-done((bf16[128,1536]{1,0:T(8,128)(2,1)S(1)}, bf16[128,1536]{1,0:T(8,128)(2,1)S(1)}, u32[]{:S(2)}, u32[]{:S(2)}) %collective-permute-start.1) | collective-permute-done | bytes 393248 | tf_op jit(solution)/shard_map/while/body/eval_jaxpr/ppermute | solution.py:18
  416.2 10.8 %conditional.6 = (bf16[128,1536]{1,0:T(8,128)(2,1)S(1)}, f32[3,1536]{1,0:T(4,128)S(1)}, bf16[1,128,1536]{2,1,0:T(8,128)(2,1)S(1)}, bf16[1,128,1536]{2,1,0:T(8,128)(2,1)S(1)}) conditional(s32[]{:T(128)} %convert_element_type.133, () %tuple.119, (pred[]{:T(512)}, s32[]{:T(128)}, bf16[4,128,1536]{2,1,0:T(8,128)(2,1)}, bf16[128,1536]{1,0:T(8,128)(2,1)S(1)}, ...), branch_computations={%region_7.7_spmd, %region_8.15_spmd} | conditional | flops 1216813952 | bytes 63521484 | solution.py:227
  429.3 12.4 %collective-permute-done.1 = bf16[128,1536]{1,0:T(8,128)(2,1)S(1)} collective-permute-done((bf16[128,1536]{1,0:T(8,128)(2,1)S(1)}, bf16[128,1536]{1,0:T(8,128)(2,1)S(1)}, u32[]{:S(2)}, u32[]{:S(2)}) %collective-permute-start.1) | collective-permute-done | bytes 393248 | tf_op jit(solution)/shard_map/while/body/eval_jaxpr/ppermute | solution.py:18
  442.9 10.8 %conditional.6 = (bf16[128,1536]{1,0:T(8,128)(2,1)S(1)}, f32[3,1536]{1,0:T(4,128)S(1)}, bf16[1,128,1536]{2,1,0:T(8,128)(2,1)S(1)}, bf16[1,128,1536]{2,1,0:T(8,128)(2,1)S(1)}) conditional(s32[]{:T(128)} %convert_element_type.133, () %tuple.119, (pred[]{:T(512)}, s32[]{:T(128)}, bf16[4,128,1536]{2,1,0:T(8,128)(2,1)}, bf16[128,1536]{1,0:T(8,128)(2,1)S(1)}, ...), branch_computations={%region_7.7_spmd, %region_8.15_spmd} | conditional | flops 1216813952 | bytes 63521484 | solution.py:227
  456.0 12.3 %collective-permute-done.1 = bf16[128,1536]{1,0:T(8,128)(2,1)S(1)} collective-permute-done((bf16[128,1536]{1,0:T(8,128)(2,1)S(1)}, bf16[128,1536]{1,0:T(8,128)(2,1)S(1)}, u32[]{:S(2)}, u32[]{:S(2)}) %collective-permute-start.1) | collective-permute-done | bytes 393248 | tf_op jit(solution)/shard_map/while/body/eval_jaxpr/ppermute | solution.py:18
  469.5 10.8 %conditional.6 = (bf16[128,1536]{1,0:T(8,128)(2,1)S(1)}, f32[3,1536]{1,0:T(4,128)S(1)}, bf16[1,128,1536]{2,1,0:T(8,128)(2,1)S(1)}, bf16[1,128,1536]{2,1,0:T(8,128)(2,1)S(1)}) conditional(s32[]{:T(128)} %convert_element_type.133, () %tuple.119, (pred[]{:T(512)}, s32[]{:T(128)}, bf16[4,128,1536]{2,1,0:T(8,128)(2,1)}, bf16[128,1536]{1,0:T(8,128)(2,1)S(1)}, ...), branch_computations={%region_7.7_spmd, %region_8.15_spmd} | conditional | flops 1216813952 | bytes 63521484 | solution.py:227
  514.4 73.1 %reduce-scatter.9.cloned.1.call-done = f32[16,48,1536]{2,1,0:T(8,128)} async-done(((f32[32,48,1536]{2,1,0:T(8,128)}), f32[16,48,1536]{2,1,0:T(8,128)}) %reduce-scatter.9.cloned.1.call-update) | async-done | bytes 4718608 | tf_op jit(solution)/shard_map/reduce_scatter | solution.py:32
  587.6 26.5 %reduce-scatter.5.cloned.1.call-done = f32[16,48,1536]{2,1,0:T(8,128)} async-done(((f32[32,48,1536]{2,1,0:T(8,128)}), f32[16,48,1536]{2,1,0:T(8,128)}) %reduce-scatter.5.cloned.1.call-update) | async-done | bytes 4718608 | tf_op jit(solution)/shard_map/reduce_scatter | solution.py:32
  614.4 14.9 %all_to_all.5 = f32[32,1,144]{2,1,0:T(1,128)S(1)} all-to-all(f32[32,1,144]{2,1,0:T(1,128)S(1)} %reshape.154), channel_id=1, replica_groups=mesh['section'=8,'dp_0'=4,'dp_1'=4,'dp_2'=2] {'dp_0','dp_1','dp_2'}, dimensions={0} | all-to-all | bytes 36864 | tf_op jit(solution)/shard_map/all_to_all | solution.py:38
  631.2 99.1 %reduce-scatter.11.cloned.1.call-done = f32[1,48,1536]{2,1,0:T(8,128)} async-done(((f32[16,48,1536]{2,1,0:T(8,128)}), f32[1,48,1536]{2,1,0:T(8,128)}) %reduce-scatter.11.cloned.1.call-update) | async-done | bytes 294928 | tf_op jit(solution)/shard_map/reduce_scatter | solution.py:33
  730.3 112.9 %reduce-scatter.7.cloned.1.call-done = f32[1,48,1536]{2,1,0:T(8,128)} async-done(((f32[16,48,1536]{2,1,0:T(8,128)}), f32[1,48,1536]{2,1,0:T(8,128)}) %reduce-scatter.7.cloned.1.call-update) | async-done | bytes 294928 | tf_op jit(solution)/shard_map/reduce_scatter | solution.py:33
  (422 shorter events, 316.9 us)
Async XLA Ops:
  7.2 580.4 %reduce-scatter.9.cloned.1.call-start = ((), (), s32[]{:S(2)}) async-start(), calls=%async_computation.7 | async-start | bytes 14155776 | tf_op jit(solution)/shard_map/reduce_scatter | solution.py:32
  41.9 8.8 %collective-permute-start = (bf16[128,1536]{1,0:T(8,128)(2,1)S(1)}, bf16[128,1536]{1,0:T(8,128)(2,1)S(1)}, u32[]{:S(2)}, u32[]{:S(2)}) collective-permute-start(bf16[128,1536]{1,0:T(8,128)(2,1)S(1)} %get-tuple-element.936), channel_id=1, source_target_pairs={{0,32},{32,64},{64,96},{96,128},{128,160},{160,192},{192,224},{1,3... | collective-permute-start | bytes 1179656 | tf_op jit(solution)/shard_map/while/body/eval_jaxpr/ppermute | solution.py:18
  77.6 9.1 %collective-permute-start = (bf16[128,1536]{1,0:T(8,128)(2,1)S(1)}, bf16[128,1536]{1,0:T(8,128)(2,1)S(1)}, u32[]{:S(2)}, u32[]{:S(2)}) collective-permute-start(bf16[128,1536]{1,0:T(8,128)(2,1)S(1)} %get-tuple-element.936), channel_id=1, source_target_pairs={{0,32},{32,64},{64,96},{96,128},{128,160},{160,192},{192,224},{1,3... | collective-permute-start | bytes 1179656 | tf_op jit(solution)/shard_map/while/body/eval_jaxpr/ppermute | solution.py:18
  90.8 15.7 %collective-permute-start = (bf16[128,1536]{1,0:T(8,128)(2,1)S(1)}, bf16[128,1536]{1,0:T(8,128)(2,1)S(1)}, u32[]{:S(2)}, u32[]{:S(2)}) collective-permute-start(bf16[128,1536]{1,0:T(8,128)(2,1)S(1)} %get-tuple-element.936), channel_id=1, source_target_pairs={{0,32},{32,64},{64,96},{96,128},{128,160},{160,192},{192,224},{1,3... | collective-permute-start | bytes 1179656 | tf_op jit(solution)/shard_map/while/body/eval_jaxpr/ppermute | solution.py:18
  110.6 14.7 %collective-permute-start = (bf16[128,1536]{1,0:T(8,128)(2,1)S(1)}, bf16[128,1536]{1,0:T(8,128)(2,1)S(1)}, u32[]{:S(2)}, u32[]{:S(2)}) collective-permute-start(bf16[128,1536]{1,0:T(8,128)(2,1)S(1)} %get-tuple-element.936), channel_id=1, source_target_pairs={{0,32},{32,64},{64,96},{96,128},{128,160},{160,192},{192,224},{1,3... | collective-permute-start | bytes 1179656 | tf_op jit(solution)/shard_map/while/body/eval_jaxpr/ppermute | solution.py:18
  129.4 14.8 %collective-permute-start = (bf16[128,1536]{1,0:T(8,128)(2,1)S(1)}, bf16[128,1536]{1,0:T(8,128)(2,1)S(1)}, u32[]{:S(2)}, u32[]{:S(2)}) collective-permute-start(bf16[128,1536]{1,0:T(8,128)(2,1)S(1)} %get-tuple-element.936), channel_id=1, source_target_pairs={{0,32},{32,64},{64,96},{96,128},{128,160},{160,192},{192,224},{1,3... | collective-permute-start | bytes 1179656 | tf_op jit(solution)/shard_map/while/body/eval_jaxpr/ppermute | solution.py:18
  148.3 14.8 %collective-permute-start = (bf16[128,1536]{1,0:T(8,128)(2,1)S(1)}, bf16[128,1536]{1,0:T(8,128)(2,1)S(1)}, u32[]{:S(2)}, u32[]{:S(2)}) collective-permute-start(bf16[128,1536]{1,0:T(8,128)(2,1)S(1)} %get-tuple-element.936), channel_id=1, source_target_pairs={{0,32},{32,64},{64,96},{96,128},{128,160},{160,192},{192,224},{1,3... | collective-permute-start | bytes 1179656 | tf_op jit(solution)/shard_map/while/body/eval_jaxpr/ppermute | solution.py:18
  167.2 19.6 %collective-permute-start = (bf16[128,1536]{1,0:T(8,128)(2,1)S(1)}, bf16[128,1536]{1,0:T(8,128)(2,1)S(1)}, u32[]{:S(2)}, u32[]{:S(2)}) collective-permute-start(bf16[128,1536]{1,0:T(8,128)(2,1)S(1)} %get-tuple-element.936), channel_id=1, source_target_pairs={{0,32},{32,64},{64,96},{96,128},{128,160},{160,192},{192,224},{1,3... | collective-permute-start | bytes 1179656 | tf_op jit(solution)/shard_map/while/body/eval_jaxpr/ppermute | solution.py:18
  190.9 14.5 %collective-permute-start = (bf16[128,1536]{1,0:T(8,128)(2,1)S(1)}, bf16[128,1536]{1,0:T(8,128)(2,1)S(1)}, u32[]{:S(2)}, u32[]{:S(2)}) collective-permute-start(bf16[128,1536]{1,0:T(8,128)(2,1)S(1)} %get-tuple-element.936), channel_id=1, source_target_pairs={{0,32},{32,64},{64,96},{96,128},{128,160},{160,192},{192,224},{1,3... | collective-permute-start | bytes 1179656 | tf_op jit(solution)/shard_map/while/body/eval_jaxpr/ppermute | solution.py:18
  209.5 19.6 %collective-permute-start = (bf16[128,1536]{1,0:T(8,128)(2,1)S(1)}, bf16[128,1536]{1,0:T(8,128)(2,1)S(1)}, u32[]{:S(2)}, u32[]{:S(2)}) collective-permute-start(bf16[128,1536]{1,0:T(8,128)(2,1)S(1)} %get-tuple-element.936), channel_id=1, source_target_pairs={{0,32},{32,64},{64,96},{96,128},{128,160},{160,192},{192,224},{1,3... | collective-permute-start | bytes 1179656 | tf_op jit(solution)/shard_map/while/body/eval_jaxpr/ppermute | solution.py:18
  233.5 15.0 %collective-permute-start.1 = (bf16[128,1536]{1,0:T(8,128)(2,1)S(1)}, bf16[128,1536]{1,0:T(8,128)(2,1)S(1)}, u32[]{:S(2)}, u32[]{:S(2)}) collective-permute-start(bf16[128,1536]{1,0:T(8,128)(2,1)S(1)} %get-tuple-element.959), channel_id=1, source_target_pairs={{32,0},{64,32},{96,64},{128,96},{160,128},{192,160},{224,192},{33,... | collective-permute-start | bytes 1179656 | tf_op jit(solution)/shard_map/while/body/eval_jaxpr/ppermute | solution.py:18
  249.9 15.1 %collective-permute-start.1 = (bf16[128,1536]{1,0:T(8,128)(2,1)S(1)}, bf16[128,1536]{1,0:T(8,128)(2,1)S(1)}, u32[]{:S(2)}, u32[]{:S(2)}) collective-permute-start(bf16[128,1536]{1,0:T(8,128)(2,1)S(1)} %get-tuple-element.959), channel_id=1, source_target_pairs={{32,0},{64,32},{96,64},{128,96},{160,128},{192,160},{224,192},{33,... | collective-permute-start | bytes 1179656 | tf_op jit(solution)/shard_map/while/body/eval_jaxpr/ppermute | solution.py:18
  266.3 15.6 %collective-permute-start.1 = (bf16[128,1536]{1,0:T(8,128)(2,1)S(1)}, bf16[128,1536]{1,0:T(8,128)(2,1)S(1)}, u32[]{:S(2)}, u32[]{:S(2)}) collective-permute-start(bf16[128,1536]{1,0:T(8,128)(2,1)S(1)} %get-tuple-element.959), channel_id=1, source_target_pairs={{32,0},{64,32},{96,64},{128,96},{160,128},{192,160},{224,192},{33,... | collective-permute-start | bytes 1179656 | tf_op jit(solution)/shard_map/while/body/eval_jaxpr/ppermute | solution.py:18
  283.3 17.2 %collective-permute-start.1 = (bf16[128,1536]{1,0:T(8,128)(2,1)S(1)}, bf16[128,1536]{1,0:T(8,128)(2,1)S(1)}, u32[]{:S(2)}, u32[]{:S(2)}) collective-permute-start(bf16[128,1536]{1,0:T(8,128)(2,1)S(1)} %get-tuple-element.959), channel_id=1, source_target_pairs={{32,0},{64,32},{96,64},{128,96},{160,128},{192,160},{224,192},{33,... | collective-permute-start | bytes 1179656 | tf_op jit(solution)/shard_map/while/body/eval_jaxpr/ppermute | solution.py:18
  301.9 20.0 %collective-permute-start.1 = (bf16[128,1536]{1,0:T(8,128)(2,1)S(1)}, bf16[128,1536]{1,0:T(8,128)(2,1)S(1)}, u32[]{:S(2)}, u32[]{:S(2)}) collective-permute-start(bf16[128,1536]{1,0:T(8,128)(2,1)S(1)} %get-tuple-element.959), channel_id=1, source_target_pairs={{32,0},{64,32},{96,64},{128,96},{160,128},{192,160},{224,192},{33,... | collective-permute-start | bytes 1179656 | tf_op jit(solution)/shard_map/while/body/eval_jaxpr/ppermute | solution.py:18
  323.3 19.8 %collective-permute-start.1 = (bf16[128,1536]{1,0:T(8,128)(2,1)S(1)}, bf16[128,1536]{1,0:T(8,128)(2,1)S(1)}, u32[]{:S(2)}, u32[]{:S(2)}) collective-permute-start(bf16[128,1536]{1,0:T(8,128)(2,1)S(1)} %get-tuple-element.959), channel_id=1, source_target_pairs={{32,0},{64,32},{96,64},{128,96},{160,128},{192,160},{224,192},{33,... | collective-permute-start | bytes 1179656 | tf_op jit(solution)/shard_map/while/body/eval_jaxpr/ppermute | solution.py:18
  344.4 43.9 %collective-permute-start.1 = (bf16[128,1536]{1,0:T(8,128)(2,1)S(1)}, bf16[128,1536]{1,0:T(8,128)(2,1)S(1)}, u32[]{:S(2)}, u32[]{:S(2)}) collective-permute-start(bf16[128,1536]{1,0:T(8,128)(2,1)S(1)} %get-tuple-element.959), channel_id=1, source_target_pairs={{32,0},{64,32},{96,64},{128,96},{160,128},{192,160},{224,192},{33,... | collective-permute-start | bytes 1179656 | tf_op jit(solution)/shard_map/while/body/eval_jaxpr/ppermute | solution.py:18
  400.3 14.6 %collective-permute-start.1 = (bf16[128,1536]{1,0:T(8,128)(2,1)S(1)}, bf16[128,1536]{1,0:T(8,128)(2,1)S(1)}, u32[]{:S(2)}, u32[]{:S(2)}) collective-permute-start(bf16[128,1536]{1,0:T(8,128)(2,1)S(1)} %get-tuple-element.959), channel_id=1, source_target_pairs={{32,0},{64,32},{96,64},{128,96},{160,128},{192,160},{224,192},{33,... | collective-permute-start | bytes 1179656 | tf_op jit(solution)/shard_map/while/body/eval_jaxpr/ppermute | solution.py:18
  427.0 14.6 %collective-permute-start.1 = (bf16[128,1536]{1,0:T(8,128)(2,1)S(1)}, bf16[128,1536]{1,0:T(8,128)(2,1)S(1)}, u32[]{:S(2)}, u32[]{:S(2)}) collective-permute-start(bf16[128,1536]{1,0:T(8,128)(2,1)S(1)} %get-tuple-element.959), channel_id=1, source_target_pairs={{32,0},{64,32},{96,64},{128,96},{160,128},{192,160},{224,192},{33,... | collective-permute-start | bytes 1179656 | tf_op jit(solution)/shard_map/while/body/eval_jaxpr/ppermute | solution.py:18
  453.7 14.5 %collective-permute-start.1 = (bf16[128,1536]{1,0:T(8,128)(2,1)S(1)}, bf16[128,1536]{1,0:T(8,128)(2,1)S(1)}, u32[]{:S(2)}, u32[]{:S(2)}) collective-permute-start(bf16[128,1536]{1,0:T(8,128)(2,1)S(1)} %get-tuple-element.959), channel_id=1, source_target_pairs={{32,0},{64,32},{96,64},{128,96},{160,128},{192,160},{224,192},{33,... | collective-permute-start | bytes 1179656 | tf_op jit(solution)/shard_map/while/body/eval_jaxpr/ppermute | solution.py:18
  480.3 8.5 %collective-permute-start.1 = (bf16[128,1536]{1,0:T(8,128)(2,1)S(1)}, bf16[128,1536]{1,0:T(8,128)(2,1)S(1)}, u32[]{:S(2)}, u32[]{:S(2)}) collective-permute-start(bf16[128,1536]{1,0:T(8,128)(2,1)S(1)} %get-tuple-element.959), channel_id=1, source_target_pairs={{32,0},{64,32},{96,64},{128,96},{160,128},{192,160},{224,192},{33,... | collective-permute-start | bytes 1179656 | tf_op jit(solution)/shard_map/while/body/eval_jaxpr/ppermute | solution.py:18
  501.0 113.0 %reduce-scatter.5.cloned.1.call-start = ((), (), s32[]{:S(2)}) async-start(), calls=%async_computation.5 | async-start | bytes 14155776 | tf_op jit(solution)/shard_map/reduce_scatter | solution.py:32
  514.4 215.9 %reduce-scatter.11.cloned.1.call-start = ((), (), s32[]{:S(2)}) async-start(), calls=%async_computation.8 | async-start | bytes 5013504 | tf_op jit(solution)/shard_map/reduce_scatter | solution.py:33
  587.6 255.6 %reduce-scatter.7.cloned.1.call-start = ((), (), s32[]{:S(2)}) async-start(), calls=%async_computation.6 | async-start | bytes 5013504 | tf_op jit(solution)/shard_map/reduce_scatter | solution.py:33
  (43 other events, 352.0 us)
Sparse Core Ops, SparseCore 0:
  501.1 86.3 reduce-scatter.8
  590.1 23.9 reduce-scatter.4
  617.2 113.0 reduce-scatter.10
  733.3 109.8 reduce-scatter.6
where the time goes:
time: 852 us; the launch traced here: 850 us
  waiting for transfers between devices  506 us (59%)
  starting transfers between devices  109 us (13%)
  local copies, waits for them, and re-layouts  105 us (12%)
  other arithmetic  45.9 us (5%)
  matrix products  39 us (5%)
  loops' own time  16.4 us (2%)
  blocking collectives  14.9 us (2%)
  between operations  13.9 us (2%)
    reduce_scatter x2, waiting for transfers between devices, sum_by_chip(): return lax.psum_scatter(parts, chips, scatter_dimension=0, tiled=True)[0]  212 us
    ppermute x22, waiting for transfers between devices, shifted(): lax.ppermute(value, axis, [(source, source + steps) for source in range(l...  194 us
    ppermute x22, starting transfers between devices, shifted(): lax.ppermute(value, axis, [(source, source + steps) for source in range(l...  109 us
    reduce_scatter x2, waiting for transfers between devices, sum_by_chip(): parts = lax.psum_scatter(parts, core, scatter_dimension=0, tiled=True)  99.6 us
    dynamic_update_slice x11, local copies, waits for them, and re-layouts, forward_tick(): saved_val = lax.dynamic_update_index_in_dim(saved_val, values, slot_id, 0)  21.3 us
    dynamic_update_slice x11, other arithmetic, forward_tick(): saved_in = lax.dynamic_update_index_in_dim(saved_in, block_in, slot_id, 0)  20.4 us
  transfers between devices with their start and end apart: 26, of which 26 were waited for; matrix products, arithmetic and copies ran while one was open for 7% of the time, Pallas kernels for 0%

commit v1 on v0

v1 whole, which is shorter than its diff:
```python
import functools
import math

import jax
import jax.numpy as jnp
from jax import lax
from jax.experimental import pallas as pl
from jax.experimental.pallas import tpu as pltpu
from jax.sharding import Mesh
from jax.sharding import PartitionSpec as P

DP = ("dp_0", "dp_1", "dp_2")
AXES = ("section",) + DP
NORM_FLOOR = 0.1
ROWS = 32
LAG = 3
MESH = pl.DeviceIdType.MESH


def conditions(guide_bin, time_step, guide_table):
    total = guide_table.shape[1]
    half = total // 2
    frequency = jnp.exp(-math.log(10000.0) * jnp.arange(half, dtype=jnp.float32) / half)
    angle = time_step.astype(jnp.float32)[..., None] * frequency
    waves = jnp.concatenate([jnp.sin(angle), jnp.cos(angle)], axis=-1)
    bin_count = guide_table.shape[0]
    onehot = (guide_bin[..., None] == jnp.arange(bin_count, dtype=jnp.int32)).astype(jnp.float32)
    picked = jnp.einsum(
        "msb,bw->msw", onehot, guide_table.astype(jnp.float32), precision=lax.Precision.HIGHEST
    )
    return picked + 0.5 * waves


def dot_plain(left, right):
    return lax.dot_general(
        left, right, (((1,), (0,)), ((), ())), preferred_element_type=jnp.float32
    )


def dot_transposed(left, right):
    return lax.dot_general(
        left, right, (((1,), (1,)), ((), ())), preferred_element_type=jnp.float32
    )


def pipeline_kernel(
    dims,
    inputs_ref,
    out_grad_ref,
    modulation_ref,
    value_ref,
    proj_ref,
    keep_mod,
    keep_val,
    keep_gp,
    keep_gv,
    table_ref,
    x_in,
    g_in,
    x_out,
    g_out,
    keep_norm,
    keep_inv,
    keep_proj,
    table_sum,
    load_sem,
    fwd_send,
    fwd_recv,
    bwd_send,
    bwd_recv,
    mirror_send,
):
    sections, zs, chunks, per_micro, rows = dims
    section = lax.axis_index("section")
    y_at = lax.axis_index("dp_0")
    z_at = lax.axis_index("dp_1")
    core = lax.axis_index("dp_2")
    last = sections - 1
    half = sections // 2
    mirrored = zs - 1 - z_at
    next_z = jnp.where(section == half - 1, mirrored, z_at)
    prev_z = jnp.where(section == half, mirrored, z_at)
    next_id = (jnp.minimum(section + 1, last), y_at, next_z, core)
    prev_id = (jnp.maximum(section - 1, 0), y_at, prev_z, core)
    mirror_id = (section, y_at, mirrored, core)

    def load(c):
        return pltpu.make_async_copy(inputs_ref.at[c], x_in.at[c], load_sem.at[c])

    def send_forward(c):
        return pltpu.make_async_remote_copy(
            src_ref=x_out.at[c],
            dst_ref=x_in.at[c],
            send_sem=fwd_send.at[c],
            recv_sem=fwd_recv.at[c],
            device_id=next_id,
            device_id_type=MESH,
        )

    def send_backward(c):
        return pltpu.make_async_remote_copy(
            src_ref=g_out.at[c],
            dst_ref=g_in.at[c],
            send_sem=bwd_send.at[c],
            recv_sem=bwd_recv.at[c],
            device_id=prev_id,
            device_id_type=MESH,
        )

    def send_mirror(c):
        return pltpu.make_async_remote_copy(
            src_ref=out_grad_ref.at[c],
            dst_ref=g_in.at[c],
            send_sem=mirror_send.at[c],
            recv_sem=bwd_recv.at[c],
            device_id=mirror_id,
            device_id_type=MESH,
        )

    @pl.when(section == 0)
    def _():
        @pl.loop(0, chunks)
        def _(c):
            load(c).start()

    barrier = pltpu.get_barrier_semaphore()

    @pl.when(section < last)
    def _():
        pl.semaphore_signal(barrier, inc=1, device_id=next_id, device_id_type=MESH)

    @pl.when(section > 0)
    def _():
        pl.semaphore_signal(barrier, inc=1, device_id=prev_id, device_id_type=MESH)

    @pl.when(section == last)
    def _():
        pl.semaphore_signal(barrier, inc=1, device_id=mirror_id, device_id_type=MESH)

    pl.semaphore_wait(barrier, jnp.where(section == 0, 1, 2))

    @pl.when(section == last)
    def _():
        @pl.loop(0, chunks)
        def _(c):
            send_mirror(c).start()

    table_sum[...] = jnp.zeros_like(table_sum)

    def forward(c):
        @pl.when(section == 0)
        def _():
            load(c).wait()

        @pl.when(section > 0)
        def _():
            send_forward(c).wait_recv()

        batch = c // per_micro
        hidden = x_in[c].astype(jnp.float32)
        centre = jnp.mean(hidden, axis=-1, keepdims=True)
        centred = hidden - centre
        spread = jnp.mean(centred * centred, axis=-1, keepdims=True)
        inverse = lax.rsqrt(spread + NORM_FLOOR)
        normed = centred * inverse
        shift = modulation_ref[batch, 0:1, :]
        scale = modulation_ref[batch, 1:2, :]
        gate = modulation_ref[batch, 2:3, :]
        modulated = (normed * scale + shift).astype(jnp.bfloat16)
        values = dot_plain(modulated, value_ref[...]).astype(jnp.bfloat16)
        projected = dot_plain(values, proj_ref[...])

        @pl.when(section < last)
        def _():
            x_out[c] = (hidden + gate * projected).astype(jnp.bfloat16)
            send_forward(c).start()

        keep_mod[c] = modulated
        keep_val[c] = values
        keep_norm[c] = normed
        keep_inv[c] = jnp.broadcast_to(inverse, (rows, 128))
        keep_proj[c] = projected

    def backward(c):
        batch = c // per_micro
        scale = modulation_ref[batch, 1:2, :]
        gate = modulation_ref[batch, 2:3, :]
        send_backward(c).wait_recv()
        grad_up = g_in[c].astype(jnp.float32)
        grad_proj = (gate * grad_up).astype(jnp.bfloat16)
        grad_values = dot_transposed(grad_proj, proj_ref[...]).astype(jnp.bfloat16)
        grad_mod = dot_transposed(grad_values, value_ref[...])
        normed = keep_norm[c]

        @pl.when(section > 0)
        def _():
            grad_norm = grad_mod * scale
            centre_grad = jnp.mean(grad_norm, axis=-1, keepdims=True)
            cross = jnp.mean(grad_norm * normed, axis=-1, keepdims=True)
            inverse = keep_inv[c][:, 0:1]
            grad_in = grad_up + inverse * (grad_norm - centre_grad - normed * cross)
            g_out[c] = grad_in.astype(jnp.bfloat16)
            send_backward(c).start()

        keep_gp[c] = grad_proj
        keep_gv[c] = grad_values
        width = grad_mod.shape[1]

        def folded(value):
            return value.reshape(rows // 8, 8, width).sum(axis=0)

        table_sum[0] += folded(grad_mod)
        table_sum[1] += folded(grad_mod * normed)
        table_sum[2] += folded(grad_up * keep_proj[c])

    lag = LAG * (last - section)

    @pl.loop(0, chunks + LAG * last)
    def _(i):
        @pl.when(i < chunks)
        def _():
            forward(i)

        c = i - lag

        @pl.when((c >= 0) & (c < chunks))
        def _():
            backward(c)

    for part in range(3):
        table_ref[part : part + 1, :] = table_sum[part].sum(axis=0, keepdims=True)

    @pl.loop(0, chunks)
    def _(c):
        @pl.when(section < last)
        def _():
            send_forward(c).wait_send()

        @pl.when(section > 0)
        def _():
            send_backward(c).wait_send()

        @pl.when(section == last)
        def _():
            send_mirror(c).wait_send()


def run_pipeline(mesh, inputs, out_grad, modulation, value_weight, proj_weight):
    batches, tok_dev, width = inputs.shape
    value_width = value_weight.shape[1]
    rows = min(ROWS, tok_dev)
    chunks = batches * tok_dev // rows
    sections = mesh.shape["section"]
    dims = (sections, mesh.shape["dp_1"], chunks, tok_dev // rows, rows)
    vmem = pl.BlockSpec(memory_space=pltpu.VMEM)
    hbm = pl.BlockSpec(memory_space=pl.ANY)
    kept = jax.ShapeDtypeStruct((chunks, rows, width), jnp.bfloat16)
    kept_val = jax.ShapeDtypeStruct((chunks, rows, value_width), jnp.bfloat16)
    dma = pltpu.SemaphoreType.DMA((chunks,))
    block = pltpu.VMEM((chunks, rows, width), jnp.bfloat16)
    wide = pltpu.VMEM((chunks, rows, width), jnp.float32)
    outs = pl.pallas_call(
        functools.partial(pipeline_kernel, dims),
        out_shape=(
            kept,
            kept_val,
            kept,
            kept_val,
            jax.ShapeDtypeStruct((3, width), jnp.float32),
        ),
        in_specs=[hbm, hbm, vmem, vmem, vmem],
        out_specs=(vmem,) * 5,
        scratch_shapes=[
            block,
            block,
            block,
            block,
            wide,
            pltpu.VMEM((chunks, rows, 128), jnp.float32),
            wide,
            pltpu.VMEM((3, 8, width), jnp.float32),
            dma,
            dma,
            dma,
            dma,
            dma,
            dma,
        ],
        compiler_params=pltpu.CompilerParams(
            collective_id=0, has_side_effects=True, vmem_limit_bytes=58 * 1024 * 1024
        ),
    )(
        inputs.reshape(chunks, rows, width),
        out_grad.reshape(chunks, rows, width),
        modulation,
        value_weight,
        proj_weight,
    )
    return outs


def split_up(value, dim, peers):
    dims = value.shape
    parts = value.reshape(*dims[:dim], peers, dims[dim] // peers, *dims[dim + 1 :])
    return jnp.moveaxis(parts, dim, 0)


def sum_by_chip(value, chips, core, dim):
    sizes = (lax.axis_size(chips), lax.axis_size(core))
    parts = split_up(value, dim, sizes[0] * sizes[1])
    inside = parts.shape[1:]
    parts = parts.reshape(*sizes, *inside).swapaxes(0, 1).reshape(-1, *inside)
    parts = lax.psum_scatter(parts, core, scatter_dimension=0, tiled=True)
    return lax.psum_scatter(parts, chips, scatter_dimension=0, tiled=True)[0]


def summed_on_arrival(value, axis, dim):
    parts = split_up(value, dim, lax.axis_size(axis))
    arrived = lax.all_to_all(parts, axis, split_axis=0, concat_axis=0, tiled=True)
    return arrived.sum(axis=0)


def contract_rows(left, right):
    left = left.reshape(-1, left.shape[-1])
    right = right.reshape(-1, right.shape[-1])
    return lax.dot_general(
        left, right, (((0,), (0,)), ((), ())), preferred_element_type=jnp.float32
    )


def per_device(
    mesh,
    inputs,
    out_grad,
    guide_bin,
    time_step,
    guide_table,
    section_table,
    value_weight,
    proj_weight,
):
    batches, tok_dev, width = inputs.shape
    assert guide_bin.shape[1] == 1
    condition = conditions(guide_bin, time_step, guide_table)
    modulation = condition[:, 0] + section_table[0].reshape(-1)
    modulation = modulation.reshape(batches, 3, width)
    modulation = modulation + jnp.array([0.0, 1.0, 0.0], jnp.float32)[None, :, None]
    keep_mod, keep_val, keep_gp, keep_gv, table_sum = run_pipeline(
        mesh, inputs, out_grad, modulation, value_weight[0], proj_weight[0]
    )
    value_full = contract_rows(keep_mod, keep_gv).astype(jnp.bfloat16)
    value_part = sum_by_chip(value_full, ("dp_0", "dp_1"), "dp_2", 0)
    proj_full = contract_rows(keep_val, keep_gp).astype(jnp.bfloat16)
    proj_part = sum_by_chip(proj_full, ("dp_0", "dp_1"), "dp_2", 0)
    table_part = summed_on_arrival(table_sum, DP, 1)
    return (
        value_part.astype(jnp.float32)[None],
        proj_part.astype(jnp.float32)[None],
        table_part[None],
    )


def solution(mesh):
    finer = Mesh(mesh.devices.reshape(mesh.shape["section"], *split_dp(mesh)), AXES)
    placed = (
        P(None, DP, None),
        P(None, DP, None),
        P(),
        P(),
        P(),
        P("section", None, None),
        P("section", None, None),
        P("section", None, None),
    )
    return jax.shard_map(
        functools.partial(per_device, finer),
        mesh=finer,
        in_specs=placed,
        out_specs=(P("section", DP, None), P("section", DP, None), P("section", None, DP)),
        check_vma=False,
    )


def split_dp(mesh):
    count = mesh.shape["dp"]
    return (4, 4, 2) if count == 32 else (1, count, 1)
```

time: 852 us -> 461 us (0.54)
  the two profiles are of different devices: /device:TPU:1 before, /device:TPU:4 now
where the time goes in v1:
time: 461 us
  waiting for transfers between devices  213 us (46%)
  Pallas kernels  195 us (42%)
  blocking collectives  15.3 us (3%)
  between operations  13.9 us (3%)
  local copies, waits for them, and re-layouts  8.85 us (2%)
  matrix products  8.27 us (2%)
  other arithmetic  6.47 us (1%)
    pallas_call x1, Pallas kernels, run_pipeline(): pl.pallas_call(functools.partial(pipeline_kernel, dims), out_shape=(kept,...  195 us
    reduce_scatter x2, waiting for transfers between devices, sum_by_chip(): return lax.psum_scatter(parts, chips, scatter_dimension=0, tiled=True)[0]  172 us
    reduce_scatter x2, waiting for transfers between devices, sum_by_chip(): parts = lax.psum_scatter(parts, core, scatter_dimension=0, tiled=True)  40.8 us
    all_to_all x1, blocking collectives, summed_on_arrival(): lax.all_to_all(parts, axis, split_axis=0, concat_axis=0, tiled=True)  15.3 us
  transfers between devices with their start and end apart: 4, of which 4 were waited for; matrix products, arithmetic and copies ran while one was open for 2% of the time, Pallas kernels for 0%

profile of v1, /device:TPU:4, one launch (start us, length us, event | category | flops | bytes accessed | tf_op | source)
XLA Modules:
  0.0 460.9 jit_solution(3071714709662927920)
XLA Ops:
  7.2 0.7 convert_bitcast_fusion
  7.9 0.7 copy.28
  8.7 0.3 multiply_sine_fusion
  9.0 0.9 convolution_add_fusion
  9.9 1.4 fusion.modulation_ref
  11.3 195.5 %shard_map.112 = (bf16[16,32,1536]{2,1,0:T(8,128)(2,1)}, bf16[16,32,1536]{2,1,0:T(8,128)(2,1)}, bf16[16,32,1536]{2,1,0:T(8,128)(2,1)}, bf16[16,32,1536]{2,1,0:T(8,128)(2,1)}, f32[3,1536]{1,0:T(4,128)}) custom-call(bf16[16,32,1536]{2,1,0:T(8,128)(2,1)} %bitcast.37, bf16[16,32,1536]{2,1,0:T(8,128)(2,1)} %bitcast.38, f32[4,3,1536]{2,1,0:T(4,128)} %fusion.modulation_ref, ...), custom_call_target="tpu_custom_call" | custom-call | tf_op jit(solution)/shard_map/pallas_call | solution.py:262
  206.8 4.5 bitcast_convert_fusion.1
  211.3 2.4 copy.18
  213.8 1.3 copy-done.2
  215.1 0.5 copy-done.3
  215.6 2.9 bitcast_convert_fusion
  218.5 2.5 copy.19
  221.0 19.0 %reduce-scatter.5.cloned.1.call-done = bf16[16,48,1536]{2,1,0:T(8,128)(2,1)} async-done(((bf16[32,48,1536]{2,1,0:T(8,128)(2,1)}), bf16[16,48,1536]{2,1,0:T(8,128)(2,1)}) %reduce-scatter.5.cloned.1.call-update) | async-done | bytes 2359312 | tf_op jit(solution)/shard_map/reduce_scatter | solution.py:313
  240.1 21.8 %reduce-scatter.9.cloned.1.call-done = bf16[16,48,1536]{2,1,0:T(8,128)(2,1)} async-done(((bf16[32,48,1536]{2,1,0:T(8,128)(2,1)}), bf16[16,48,1536]{2,1,0:T(8,128)(2,1)}) %reduce-scatter.9.cloned.1.call-update) | async-done | bytes 2359312 | tf_op jit(solution)/shard_map/reduce_scatter | solution.py:313
  262.1 0.1 reshape.100
  262.2 15.3 %all_to_all.5 = f32[32,1,144]{2,1,0:T(1,128)S(1)} all-to-all(f32[32,1,144]{2,1,0:T(1,128)S(1)} %reshape.100), channel_id=1, replica_groups=mesh['section'=8,'dp_0'=4,'dp_1'=4,'dp_2'=2] {'dp_0','dp_1','dp_2'}, dimensions={0} | all-to-all | bytes 36864 | tf_op jit(solution)/shard_map/all_to_all | solution.py:319
  277.5 0.5 broadcast.31
  278.0 0.7 reduce
  278.7 0.1 reshape.101
  278.9 0.6 broadcast_in_dim.2
  279.4 80.3 %reduce-scatter.7.cloned.1.call-done = bf16[1,48,1536]{2,1,0:T(8,128)(2,1)} async-done(((bf16[16,48,1536]{2,1,0:T(8,128)(2,1)}), bf16[1,48,1536]{2,1,0:T(8,128)(2,1)}) %reduce-scatter.7.cloned.1.call-update) | async-done | bytes 147472 | tf_op jit(solution)/shard_map/reduce_scatter | solution.py:314
  359.8 1.6 convert_element_type.21
  361.4 91.3 %reduce-scatter.11.cloned.1.call-done = bf16[1,48,1536]{2,1,0:T(8,128)(2,1)} async-done(((bf16[16,48,1536]{2,1,0:T(8,128)(2,1)}), bf16[1,48,1536]{2,1,0:T(8,128)(2,1)}) %reduce-scatter.11.cloned.1.call-update) | async-done | bytes 147472 | tf_op jit(solution)/shard_map/reduce_scatter | solution.py:314
  452.7 1.6 convert_element_type.23
  (18 shorter events, 0.4 us)
Async XLA Ops:
  7.2 1.8 copy-start
  7.2 232.9 %reduce-scatter.5.cloned.1.call-start = ((), (), s32[]{:S(2)}) async-start(), calls=%async_computation.5 | async-start | bytes 7077888 | tf_op jit(solution)/shard_map/reduce_scatter | solution.py:313
  213.7 1.4 copy-start.2
  213.7 1.9 copy-start.3
  213.7 48.2 %reduce-scatter.9.cloned.1.call-start = ((), (), s32[]{:S(2)}) async-start(), calls=%async_computation.7 | async-start | bytes 7077888 | tf_op jit(solution)/shard_map/reduce_scatter | solution.py:313
  221.0 138.8 %reduce-scatter.7.cloned.1.call-start = ((), (), s32[]{:S(2)}) async-start(), calls=%async_computation.6 | async-start | bytes 2506752 | tf_op jit(solution)/shard_map/reduce_scatter | solution.py:314
  240.1 21.9 %copy-start.1 = (f32[3,1536]{1,0:T(4,128)S(1)}, f32[3,1536]{1,0:T(4,128)}, u32[]{:S(2)}) copy-start(f32[3,1536]{1,0:T(4,128)} %get-tuple-element.12) | copy-start | bytes 55300
  240.1 212.7 %reduce-scatter.11.cloned.1.call-start = ((), (), s32[]{:S(2)}) async-start(), calls=%async_computation.8 | async-start | bytes 2506752 | tf_op jit(solution)/shard_map/reduce_scatter | solution.py:314
Sparse Core Ops, SparseCore 0:
  213.9 26.1 reduce-scatter.4
  242.6 19.2 reduce-scatter.8
  264.5 95.2 reduce-scatter.6
  362.2 90.5 reduce-scatter.10

commit v2 on v1

v2 whole, which is shorter than its diff:
```python
import functools
import math

import jax
import jax.numpy as jnp
from jax import lax
from jax.experimental import pallas as pl
from jax.experimental.pallas import tpu as pltpu
from jax.sharding import Mesh
from jax.sharding import PartitionSpec as P

DP = ("dp_0", "dp_1", "dp_2")
AXES = ("section",) + DP
NORM_FLOOR = 0.1
ROWS = 32
LAG = 3
VMEM_LIMIT = 63 * 1024 * 1024
MESH = pl.DeviceIdType.MESH


def conditions(guide_bin, time_step, guide_table):
    total = guide_table.shape[1]
    half = total // 2
    frequency = jnp.exp(-math.log(10000.0) * jnp.arange(half, dtype=jnp.float32) / half)
    angle = time_step.astype(jnp.float32)[..., None] * frequency
    waves = jnp.concatenate([jnp.sin(angle), jnp.cos(angle)], axis=-1)
    bin_count = guide_table.shape[0]
    onehot = (guide_bin[..., None] == jnp.arange(bin_count, dtype=jnp.int32)).astype(jnp.float32)
    picked = jnp.einsum(
        "msb,bw->msw", onehot, guide_table.astype(jnp.float32), precision=lax.Precision.HIGHEST
    )
    return picked + 0.5 * waves


def dot_plain(left, right):
    return lax.dot_general(
        left, right, (((1,), (0,)), ((), ())), preferred_element_type=jnp.float32
    )


def dot_transposed(left, right):
    return lax.dot_general(
        left, right, (((1,), (1,)), ((), ())), preferred_element_type=jnp.float32
    )


def pipeline_kernel(
    dims,
    inputs_ref,
    out_grad_ref,
    modulation_ref,
    value_ref,
    proj_ref,
    value_out,
    proj_out,
    table_out,
    x_in,
    g_in,
    x_out,
    g_out,
    keep_mod,
    keep_val,
    keep_norm,
    keep_inv,
    keep_proj,
    own_grad,
    peer_grad,
    turned,
    peer_turned,
    table_sum,
    table_now,
    table_got,
    first_stage,
    first_got,
    second_stage,
    second_got,
    far_stage,
    far_got,
    own_sum,
    load_sem,
    fwd_send,
    fwd_recv,
    bwd_send,
    bwd_recv,
    mirror_send,
    grad_send,
    grad_recv,
    turn_send,
    turn_recv,
    first_send,
    first_recv,
    second_send,
    second_recv,
    far_send,
    far_recv,
    table_send,
    table_recv,
):
    sections, ys, zs, cores, chunks, per_micro, rows = dims
    section = lax.axis_index("section")
    y_at = lax.axis_index("dp_0")
    z_at = lax.axis_index("dp_1")
    core = lax.axis_index("dp_2")
    last = sections - 1
    half = sections // 2
    batches = chunks // per_micro
    tok_micro = per_micro * rows
    width = x_in.shape[2]
    tall = own_sum.shape[3]
    mirrored = zs - 1 - z_at
    next_z = jnp.where(section == half - 1, mirrored, z_at)
    prev_z = jnp.where(section == half, mirrored, z_at)
    next_id = (jnp.minimum(section + 1, last), y_at, next_z, core)
    prev_id = (jnp.maximum(section - 1, 0), y_at, prev_z, core)
    mirror_id = (section, y_at, mirrored, core)
    peer_id = (section, y_at, z_at, 1 - core)

    def y_id(step):
        return (section, (y_at + step + ys) % ys, z_at, core)

    def z_id(step):
        return (section, y_at, (z_at + step + zs) % zs, core)

    def remote(src, dst, send_sem, recv_sem, device_id):
        return pltpu.make_async_remote_copy(
            src_ref=src,
            dst_ref=dst,
            send_sem=send_sem,
            recv_sem=recv_sem,
            device_id=device_id,
            device_id_type=MESH,
        )

    def load(c):
        return pltpu.make_async_copy(inputs_ref.at[c], x_in.at[c], load_sem.at[c])

    def send_forward(c):
        return remote(x_out.at[c], x_in.at[c], fwd_send.at[c], fwd_recv.at[c], next_id)

    def send_backward(c):
        return remote(g_out.at[c], g_in.at[c], bwd_send.at[c], bwd_recv.at[c], prev_id)

    def send_mirror(c):
        return remote(out_grad_ref.at[c], g_in.at[c], mirror_send.at[c], bwd_recv.at[c], mirror_id)

    def share_grad(kind, c):
        at = pl.ds(pl.multiple_of(c * rows, rows), rows)
        return remote(
            own_grad.at[kind, at],
            peer_grad.at[kind, at],
            grad_send.at[kind, c],
            grad_recv.at[kind, c],
            peer_id,
        )

    def share_turned(kind):
        return remote(
            turned.at[kind, 1 - core],
            peer_turned.at[kind],
            turn_send.at[kind],
            turn_recv.at[kind],
            peer_id,
        )

    @pl.when(section == 0)
    def _():
        @pl.loop(0, chunks)
        def _(c):
            load(c).start()

    barrier = pltpu.get_barrier_semaphore()

    def greet(device_id):
        pl.semaphore_signal(barrier, inc=1, device_id=device_id, device_id_type=MESH)

    @pl.when(section < last)
    def _():
        greet(next_id)

    @pl.when(section > 0)
    def _():
        greet(prev_id)

    @pl.when(section == last)
    def _():
        greet(mirror_id)

    greet(peer_id)
    for step in range(1, ys):
        greet(y_id(step))
    for step in range(1, zs):
        greet(z_id(step))
    pl.semaphore_wait(barrier, jnp.where(section == 0, 1, 2) + ys + zs - 1)

    @pl.when(section == last)
    def _():
        @pl.loop(0, chunks)
        def _(c):
            send_mirror(c).start()

    table_sum[...] = jnp.zeros_like(table_sum)

    def forward(c):
        @pl.when(section == 0)
        def _():
            load(c).wait()

        @pl.when(section > 0)
        def _():
            send_forward(c).wait_recv()

        batch = c // per_micro
        hidden = x_in[c].astype(jnp.float32)
        centre = jnp.mean(hidden, axis=-1, keepdims=True)
        centred = hidden - centre
        spread = jnp.mean(centred * centred, axis=-1, keepdims=True)
        inverse = lax.rsqrt(spread + NORM_FLOOR)
        normed = centred * inverse
        shift = modulation_ref[batch, 0:1, :]
        scale = modulation_ref[batch, 1:2, :]
        gate = modulation_ref[batch, 2:3, :]
        modulated = (normed * scale + shift).astype(jnp.bfloat16)
        values = dot_plain(modulated, value_ref[...]).astype(jnp.bfloat16)
        projected = dot_plain(values, proj_ref[...])

        @pl.when(section < last)
        def _():
            x_out[c] = (hidden + gate * projected).astype(jnp.bfloat16)
            send_forward(c).start()

        keep_mod[c] = modulated
        keep_val[c] = values
        keep_norm[c] = normed
        keep_inv[c] = jnp.broadcast_to(inverse, (rows, 128))
        keep_proj[c] = projected

    def backward(c):
        batch = c // per_micro
        at = pl.ds(pl.multiple_of(c * rows, rows), rows)
        scale = modulation_ref[batch, 1:2, :]
        gate = modulation_ref[batch, 2:3, :]
        send_backward(c).wait_recv()
        grad_up = g_in[c].astype(jnp.float32)
        grad_proj = (gate * grad_up).astype(jnp.bfloat16)
        grad_values = dot_transposed(grad_proj, proj_ref[...]).astype(jnp.bfloat16)
        grad_mod = dot_transposed(grad_values, value_ref[...])
        normed = keep_norm[c]

        @pl.when(section > 0)
        def _():
            grad_norm = grad_mod * scale
            centre_grad = jnp.mean(grad_norm, axis=-1, keepdims=True)
            cross = jnp.mean(grad_norm * normed, axis=-1, keepdims=True)
            inverse = keep_inv[c][:, 0:1]
            grad_in = grad_up + inverse * (grad_norm - centre_grad - normed * cross)
            g_out[c] = grad_in.astype(jnp.bfloat16)
            send_backward(c).start()

        own_grad[0, at] = grad_values
        own_grad[1, at] = grad_proj
        share_grad(0, c).start()
        share_grad(1, c).start()

        def folded(value):
            return value.reshape(rows // 8, 8, width).sum(axis=0)

        table_sum[0] += folded(grad_mod)
        table_sum[1] += folded(grad_mod * normed)
        table_sum[2] += folded(grad_up * keep_proj[c])

    def turn():
        for kind, keep in ((0, keep_mod), (1, keep_val)):
            for batch in range(batches):
                part = keep[pl.ds(batch * per_micro, per_micro)].reshape(tok_micro, width)
                flipped = part.T.reshape(ys, zs, cores, tall, tok_micro)
                for z in range(zs):
                    for to in range(cores):
                        turned[kind, to, z, :, :, pl.ds(batch * tok_micro, tok_micro)] = flipped[
                            :, z, to
                        ]
            share_turned(kind).start()

    lag = LAG * (last - section)
    turn_at = jnp.where(lag >= chunks, chunks, chunks + lag)

    @pl.loop(0, chunks + LAG * last + 1)
    def _(i):
        @pl.when(i < chunks)
        def _():
            forward(i)

        @pl.when(i == turn_at)
        def _():
            turn()

        c = i - lag

        @pl.when((c >= 0) & (c < chunks))
        def _():
            backward(c)

    table_now[...] = jnp.zeros_like(table_now)
    for part in range(3):
        table_now[0, part : part + 1, :] = table_sum[part].sum(axis=0, keepdims=True)

    def share_table(stage, slot, device_id):
        return remote(
            table_now.at[stage],
            table_got.at[slot],
            table_send.at[slot],
            table_recv.at[slot],
            device_id,
        )

    table_moves = [[share_table(0, 0, peer_id)]]
    table_moves.append([share_table(1, step, y_id(step)) for step in range(1, ys)])
    table_moves.append([share_table(2, ys + step - 1, z_id(step)) for step in range(1, zs)])

    def table_step(stage):
        total = table_now[stage]
        for move in table_moves[stage]:
            move.wait_recv()
        for slot in {0: [0], 1: range(1, ys), 2: range(ys, ys + zs - 1)}[stage]:
            total = total + table_got[slot]
        table_now[stage + 1] = total
        if stage < 2:
            for move in table_moves[stage + 1]:
                move.start()

    for move in table_moves[0]:
        move.start()

    @pl.loop(0, chunks)
    def _(c):
        share_grad(0, c).wait_recv()
        share_grad(1, c).wait_recv()

    share_turned(0).wait_recv()
    share_turned(1).wait_recv()

    def z_of(seg):
        return (z_at + 2 * zs - 1 - seg) % zs

    ahead = (y_at + 1) % ys
    behind = (y_at + ys - 1) % ys
    across = (y_at + 2) % ys
    toward = (1, -1)

    def first_move(seg, kind):
        return remote(
            first_stage.at[seg, kind],
            first_got.at[seg, kind],
            first_send.at[seg, kind],
            first_recv.at[seg, kind],
            y_id(toward[kind]),
        )

    def second_move(seg, kind, way):
        return remote(
            second_stage.at[seg, kind, way],
            second_got.at[seg, kind, way],
            second_send.at[seg, kind, way],
            second_recv.at[seg, kind, way],
            y_id(toward[way]),
        )

    def far_move(seg, kind):
        return remote(
            far_stage.at[seg, kind],
            far_got.at[seg, kind],
            far_send.at[seg, kind],
            far_recv.at[seg, kind],
            z_id(-1 - seg),
        )

    def compute(seg):
        z_to = z_of(seg)
        for kind in range(2):
            left = turned[kind, core, z_to].reshape(ys * tall, -1)
            left_peer = peer_turned[kind, z_to].reshape(ys * tall, -1)
            block = dot_plain(left, own_grad[kind]) + dot_plain(left_peer, peer_grad[kind])
            own_sum[seg, kind] = block.reshape(ys, tall, width)
            first_stage[seg, kind] = own_sum[seg, kind, across].astype(jnp.bfloat16)
            first_move(seg, kind).start()

    def second(seg):
        for kind in range(2):
            for way, to in ((0, ahead), (1, behind)):
                if way != kind:
                    second_stage[seg, kind, way] = own_sum[seg, kind, to].astype(jnp.bfloat16)
                    second_move(seg, kind, way).start()
        for kind, to in ((0, ahead), (1, behind)):
            first_move(seg, kind).wait_recv()
            total = own_sum[seg, kind, to] + first_got[seg, kind].astype(jnp.float32)
            second_stage[seg, kind, kind] = total.astype(jnp.bfloat16)
            second_move(seg, kind, kind).start()

    def third(seg):
        for kind in range(2):
            total = own_sum[seg, kind, y_at]
            for way in range(2):
                second_move(seg, kind, way).wait_recv()
                total = total + second_got[seg, kind, way].astype(jnp.float32)
            if seg < zs - 1:
                far_stage[seg, kind] = total.astype(jnp.bfloat16)
                far_move(seg, kind).start()
            else:
                own_sum[seg, kind, y_at] = total

    compute(0)
    for seg in range(zs):
        if seg + 1 < zs:
            compute(seg + 1)
        second(seg)
        if seg > 0:
            third(seg - 1)
        if seg == 0:
            table_step(0)
        if seg == zs - 1:
            table_step(1)
    third(zs - 1)
    table_step(2)
    me = (y_at * zs + z_at) * cores + core
    table = table_now[3]
    mine = jnp.zeros((8, tall), jnp.float32)
    for owner in range(ys * zs * cores):
        mine = mine + jnp.where(me == owner, table[:, owner * tall : (owner + 1) * tall], 0.0)
    table_out[...] = mine[:3]
    for kind, out in ((0, value_out), (1, proj_out)):
        total = own_sum[zs - 1, kind, y_at]
        for seg in range(zs - 1):
            far_move(seg, kind).wait_recv()
            total = total + far_got[seg, kind].astype(jnp.float32)
        out[...] = total

    for seg in range(zs):
        for kind in range(2):
            first_move(seg, kind).wait_send()
            second_move(seg, kind, 0).wait_send()
            second_move(seg, kind, 1).wait_send()
            if seg < zs - 1:
                far_move(seg, kind).wait_send()
    for moves in table_moves:
        for move in moves:
            move.wait_send()
    share_turned(0).wait_send()
    share_turned(1).wait_send()

    @pl.loop(0, chunks)
    def _(c):
        share_grad(0, c).wait_send()
        share_grad(1, c).wait_send()

        @pl.when(section < last)
        def _():
            send_forward(c).wait_send()

        @pl.when(section > 0)
        def _():
            send_backward(c).wait_send()

        @pl.when(section == last)
        def _():
            send_mirror(c).wait_send()


def run_pipeline(mesh, inputs, out_grad, modulation, value_weight, proj_weight):
    batches, tok_dev, width = inputs.shape
    value_width = value_weight.shape[1]
    assert value_width == width
    rows = min(ROWS, tok_dev)
    chunks = batches * tok_dev // rows
    tokens = batches * tok_dev
    sections = mesh.shape["section"]
    ys, zs, cores = (mesh.shape[name] for name in DP)
    tall = width // (ys * zs * cores)
    dims = (sections, ys, zs, cores, chunks, tok_dev // rows, rows)
    vmem = pl.BlockSpec(memory_space=pltpu.VMEM)
    hbm = pl.BlockSpec(memory_space=pl.ANY)
    half, full = jnp.bfloat16, jnp.float32

    def sems(*shape):
        return pltpu.SemaphoreType.DMA(shape)

    return pl.pallas_call(
        functools.partial(pipeline_kernel, dims),
        out_shape=(
            jax.ShapeDtypeStruct((tall, width), full),
            jax.ShapeDtypeStruct((tall, width), full),
            jax.ShapeDtypeStruct((3, tall), full),
        ),
        in_specs=[hbm, hbm, vmem, vmem, vmem],
        out_specs=(vmem,) * 3,
        scratch_shapes=[
            pltpu.VMEM((chunks, rows, width), half),
            pltpu.VMEM((chunks, rows, width), half),
            pltpu.VMEM((chunks, rows, width), half),
            pltpu.VMEM((chunks, rows, width), half),
            pltpu.VMEM((chunks, rows, width), half),
            pltpu.VMEM((chunks, rows, width), half),
            pltpu.VMEM((chunks, rows, width), full),
            pltpu.VMEM((chunks, rows, 128), full),
            pltpu.VMEM((chunks, rows, width), full),
            pltpu.VMEM((2, tokens, width), half),
            pltpu.VMEM((2, tokens, width), half),
            pltpu.VMEM((2, cores, zs, ys, tall, tokens), half),
            pltpu.VMEM((2, zs, ys, tall, tokens), half),
            pltpu.VMEM((3, 8, width), full),
            pltpu.VMEM((4, 8, width), full),
            pltpu.VMEM((ys + zs - 1, 8, width), full),
            pltpu.VMEM((zs, 2, tall, width), half),
            pltpu.VMEM((zs, 2, tall, width), half),
            pltpu.VMEM((zs, 2, 2, tall, width), half),
            pltpu.VMEM((zs, 2, 2, tall, width), half),
            pltpu.VMEM((zs - 1, 2, tall, width), half),
            pltpu.VMEM((zs - 1, 2, tall, width), half),
            pltpu.VMEM((zs, 2, ys, tall, width), full),
            sems(chunks),
            sems(chunks),
            sems(chunks),
            sems(chunks),
            sems(chunks),
            sems(chunks),
            sems(2, chunks),
            sems(2, chunks),
            sems(2),
            sems(2),
            sems(zs, 2),
            sems(zs, 2),
            sems(zs, 2, 2),
            sems(zs, 2, 2),
            sems(zs - 1, 2),
            sems(zs - 1, 2),
            sems(ys + zs - 1),
            sems(ys + zs - 1),
        ],
        compiler_params=pltpu.CompilerParams(
            collective_id=0, has_side_effects=True, vmem_limit_bytes=VMEM_LIMIT
        ),
    )(
        inputs.reshape(chunks, rows, width),
        out_grad.reshape(chunks, rows, width),
        modulation,
        value_weight,
        proj_weight,
    )


def per_device(
    mesh,
    inputs,
    out_grad,
    guide_bin,
    time_step,
    guide_table,
    section_table,
    value_weight,
    proj_weight,
):
    batches, tok_dev, width = inputs.shape
    assert guide_bin.shape[1] == 1
    condition = conditions(guide_bin, time_step, guide_table)
    modulation = condition[:, 0] + section_table[0].reshape(-1)
    modulation = modulation.reshape(batches, 3, width)
    modulation = modulation + jnp.array([0.0, 1.0, 0.0], jnp.float32)[None, :, None]
    value_part, proj_part, table_part = run_pipeline(
        mesh, inputs, out_grad, modulation, value_weight[0], proj_weight[0]
    )
    return (value_part[None], proj_part[None], table_part[None])


def solution(mesh):
    finer = Mesh(mesh.devices.reshape(mesh.shape["section"], *split_dp(mesh)), AXES)
    placed = (
        P(None, DP, None),
        P(None, DP, None),
        P(),
        P(),
        P(),
        P("section", None, None),
        P("section", None, None),
        P("section", None, None),
    )
    return jax.shard_map(
        functools.partial(per_device, finer),
        mesh=finer,
        in_specs=placed,
        out_specs=(P("section", DP, None), P("section", DP, None), P("section", None, DP)),
        check_vma=False,
    )


def split_dp(mesh):
    count = mesh.shape["dp"]
    return (4, 4, 2) if count == 32 else (1, count, 1)
```

time: 461 us -> 269 us (0.58)
  the two profiles are of different devices: /device:TPU:4 before, /device:TPU:1 now
where the time goes in v2:
time: 269 us
  Pallas kernels  260 us (97%)
  local copies, waits for them, and re-layouts  5.37 us (2%)
    pallas_call x1, Pallas kernels, run_pipeline(): pl.pallas_call(functools.partial(pipeline_kernel, dims), out_shape=(jax.S...  260 us

profile of v2, /device:TPU:1, one launch (start us, length us, event | category | flops | bytes accessed | tf_op | source)
XLA Modules:
  0.0 269.0 jit_solution(5593454100758347365)
XLA Ops:
  0.6 0.0 copy-start
  0.6 0.7 convert_bitcast_fusion
  1.4 0.7 copy.20
  2.1 0.3 multiply_sine_fusion
  2.4 0.0 copy-done
  2.4 0.9 convolution_add_fusion
  3.3 1.4 fusion.modulation_ref
  4.7 259.7 %shard_map.112 = (f32[48,1536]{1,0:T(8,128)}, f32[48,1536]{1,0:T(8,128)}, f32[3,48]{1,0:T(4,128)}) custom-call(bf16[16,32,1536]{2,1,0:T(8,128)(2,1)} %bitcast.17, bf16[16,32,1536]{2,1,0:T(8,128)(2,1)} %bitcast.18, f32[4,3,1536]{2,1,0:T(4,128)} %fusion.modulation_ref, bf16[1536,1536]{1,0:T(8,128)(2,1)} %bitcast.15, bf16[1536,1536]{1,0:T(8,128)(2,1)} %bitcast.16), custom_call_target="tpu_custom_call" | custom-call | tf_op jit(solution)/shard_map/pallas_call | solution.py:485
  264.4 1.2 copy.14
  265.6 1.7 copy.23
  267.3 1.7 copy.24
  (1 shorter events, 0.0 us)
Async XLA Ops:
  0.6 1.8 copy-start

commit v3 on v2

--- a/solution.py
+++ b/solution.py
@@ -14,22 +14,9 @@
 NORM_FLOOR = 0.1
 ROWS = 32
 LAG = 3
-VMEM_LIMIT = 63 * 1024 * 1024
+RELAY_LAG = 8
+VMEM_LIMIT = 67043328
 MESH = pl.DeviceIdType.MESH
-
-
-def conditions(guide_bin, time_step, guide_table):
-    total = guide_table.shape[1]
-    half = total // 2
-    frequency = jnp.exp(-math.log(10000.0) * jnp.arange(half, dtype=jnp.float32) / half)
-    angle = time_step.astype(jnp.float32)[..., None] * frequency
-    waves = jnp.concatenate([jnp.sin(angle), jnp.cos(angle)], axis=-1)
-    bin_count = guide_table.shape[0]
-    onehot = (guide_bin[..., None] == jnp.arange(bin_count, dtype=jnp.int32)).astype(jnp.float32)
-    picked = jnp.einsum(
-        "msb,bw->msw", onehot, guide_table.astype(jnp.float32), precision=lax.Precision.HIGHEST
-    )
-    return picked + 0.5 * waves
 
 
 def dot_plain(left, right):
@@ -38,19 +25,16 @@
     )
 
 
-def dot_transposed(left, right):
-    return lax.dot_general(
-        left, right, (((1,), (1,)), ((), ())), preferred_element_type=jnp.float32
-    )
-
-
 def pipeline_kernel(
     dims,
     inputs_ref,
     out_grad_ref,
-    modulation_ref,
-    value_ref,
-    proj_ref,
+    bin_ref,
+    step_ref,
+    guide_ref,
+    section_ref,
+    value_hbm,
+    proj_hbm,
     value_out,
     proj_out,
     table_out,
@@ -58,8 +42,12 @@
     g_in,
     x_out,
     g_out,
-    keep_mod,
-    keep_val,
+    value_ref,
+    proj_ref,
+    value_turned,
+    proj_turned,
+    modulation_ref,
+    pool,
     keep_norm,
     keep_inv,
     keep_proj,
@@ -72,17 +60,21 @@
     table_got,
     first_stage,
     first_got,
-    second_stage,
     second_got,
     far_stage,
     far_got,
+    fresh,
+    partial,
     own_sum,
     load_sem,
+    weight_sem,
     fwd_send,
     fwd_recv,
     bwd_send,
     bwd_recv,
     mirror_send,
+    relay_send,
+    relay_recv,
     grad_send,
     grad_recv,
     turn_send,
@@ -106,7 +98,8 @@
     batches = chunks // per_micro
     tok_micro = per_micro * rows
     width = x_in.shape[2]
-    tall = own_sum.shape[3]
+    tall = own_sum.shape[2]
+    tokens = chunks * rows
     mirrored = zs - 1 - z_at
     next_z = jnp.where(section == half - 1, mirrored, z_at)
     prev_z = jnp.where(section == half, mirrored, z_at)
@@ -114,6 +107,15 @@
     prev_id = (jnp.maximum(section - 1, 0), y_at, prev_z, core)
     mirror_id = (section, y_at, mirrored, core)
     peer_id = (section, y_at, z_at, 1 - core)
+    inner = (z_at > 0) & (z_at < zs - 1)
+    hop_out = inner & (section == half - 1)
+    hop_back = inner & (section == half)
+    relay_out = inner & (section == 0)
+    relay_back = inner & (section == last)
+    first_id = (0, y_at, z_at, core)
+    last_id = (last, y_at, z_at, core)
+    cross_out = (half, y_at, mirrored, core)
+    cross_back = (half - 1, y_at, mirrored, core)
 
     def y_id(step):
         return (section, (y_at + step + ys) % ys, z_at, core)
@@ -140,6 +142,18 @@
     def send_backward(c):
         return remote(g_out.at[c], g_in.at[c], bwd_send.at[c], bwd_recv.at[c], prev_id)
 
+    def hop_forward(c):
+        return remote(x_out.at[c], g_out.at[c], fwd_send.at[c], relay_recv.at[c], first_id)
+
+    def hop_backward(c):
+        return remote(g_out.at[c], x_out.at[c], bwd_send.at[c], relay_recv.at[c], last_id)
+
+    def relay_forward(c):
+        return remote(g_out.at[c], x_in.at[c], relay_send.at[c], fwd_recv.at[c], cross_out)
+
+    def relay_backward(c):
+        return remote(x_out.at[c], g_in.at[c], relay_send.at[c], bwd_recv.at[c], cross_back)
+
     def send_mirror(c):
         return remote(out_grad_ref.at[c], g_in.at[c], mirror_send.at[c], bwd_recv.at[c], mirror_id)
 
@@ -162,6 +176,11 @@
             peer_id,
         )
 
+    load_value = pltpu.make_async_copy(value_hbm, value_ref, weight_sem.at[0])
+    load_proj = pltpu.make_async_copy(proj_hbm, proj_ref, weight_sem.at[1])
+    load_value.start()
+    load_proj.start()
+
     @pl.when(section == 0)
     def _():
         @pl.loop(0, chunks)
@@ -185,12 +204,60 @@
     def _():
         greet(mirror_id)
 
+    @pl.when(relay_out)
+    def _():
+        greet((half - 1, y_at, z_at, core))
+        greet(cross_out)
+
+    @pl.when(hop_out)
+    def _():
+        greet(first_id)
+        greet((last, y_at, mirrored, core))
+
+    @pl.when(hop_back)
+    def _():
+        greet(last_id)
+        greet((0, y_at, mirrored, core))
+
+    @pl.when(relay_back)
+    def _():
+        greet((half, y_at, z_at, core))
+        greet(cross_back)
+
+    relays = relay_out | hop_out | hop_back | relay_back
     greet(peer_id)
     for step in range(1, ys):
         greet(y_id(step))
     for step in range(1, zs):
         greet(z_id(step))
-    pl.semaphore_wait(barrier, jnp.where(section == 0, 1, 2) + ys + zs - 1)
+    half_wave = 3 * width // 2
+    row_at = lax.broadcasted_iota(jnp.int32, (8, half_wave), 0)
+    lane_at = lax.broadcasted_iota(jnp.int32, (8, half_wave), 1).astype(jnp.float32)
+    angle = jnp.exp(-math.log(10000.0) * lane_at / half_wave)
+    bin_at = lax.broadcasted_iota(jnp.int32, (8, guide_ref.shape[0]), 1)
+    bin_row = lax.broadcasted_iota(jnp.int32, (8, guide_ref.shape[0]), 0)
+    step = jnp.zeros((8, half_wave), jnp.float32)
+    onehot = jnp.zeros(bin_at.shape, jnp.float32)
+    for batch in range(batches):
+        step = jnp.where(row_at == batch, step_ref[batch, 0].astype(jnp.float32), step)
+        hit = (bin_row == batch) & (bin_at == bin_ref[batch, 0])
+        onehot = jnp.where(hit, 1.0, onehot)
+    angle = step * angle
+    picked = dot_plain(onehot.astype(jnp.bfloat16), guide_ref[...])
+    modulation_ref[:, :half_wave] = picked[:, :half_wave] + 0.5 * jnp.sin(angle)
+    modulation_ref[:, half_wave:] = picked[:, half_wave:] + 0.5 * jnp.cos(angle)
+    for part in range(3):
+        at = pl.ds(part * width, width)
+        row = section_ref[part : part + 1, :]
+        if part == 1:
+            row = row + 1.0
+        modulation_ref[:, at] = modulation_ref[:, at] + row
+
+    def modulation(batch):
+        whole = modulation_ref[pl.ds(batch, 1), :]
+        return whole[:, :width], whole[:, width : 2 * width], whole[:, 2 * width :]
+
+    pl.semaphore_wait(barrier, jnp.where(section == 0, 1, 2) + jnp.where(relays, 2, 0) + ys + zs - 1)
 
     @pl.when(section == last)
     def _():
@@ -216,9 +283,7 @@
         spread = jnp.mean(centred * centred, axis=-1, keepdims=True)
         inverse = lax.rsqrt(spread + NORM_FLOOR)
         normed = centred * inverse
-        shift = modulation_ref[batch, 0:1, :]
-        scale = modulation_ref[batch, 1:2, :]
-        gate = modulation_ref[batch, 2:3, :]
+        shift, scale, gate = modulation(batch)
         modulated = (normed * scale + shift).astype(jnp.bfloat16)
         values = dot_plain(modulated, value_ref[...]).astype(jnp.bfloat16)
         projected = dot_plain(values, proj_ref[...])
@@ -226,10 +291,17 @@
         @pl.when(section < last)
         def _():
             x_out[c] = (hidden + gate * projected).astype(jnp.bfloat16)
+
+        @pl.when((section < last) & ~hop_out)
+        def _():
             send_forward(c).start()
 
-        keep_mod[c] = modulated
-        keep_val[c] = values
+        @pl.when(hop_out)
+        def _():
+            hop_forward(c).start()
+
+        pool[pl.ds(pl.multiple_of(c * rows, rows), rows)] = modulated
+        pool[pl.ds(pl.multiple_of(tokens + c * rows, rows), rows)] = values
         keep_norm[c] = normed
         keep_inv[c] = jnp.broadcast_to(inverse, (rows, 128))
         keep_proj[c] = projected
@@ -237,13 +309,12 @@
     def backward(c):
         batch = c // per_micro
         at = pl.ds(pl.multiple_of(c * rows, rows), rows)
-        scale = modulation_ref[batch, 1:2, :]
-        gate = modulation_ref[batch, 2:3, :]
+        unused, scale, gate = modulation(batch)
         send_backward(c).wait_recv()
         grad_up = g_in[c].astype(jnp.float32)
         grad_proj = (gate * grad_up).astype(jnp.bfloat16)
-        grad_values = dot_transposed(grad_proj, proj_ref[...]).astype(jnp.bfloat16)
-        grad_mod = dot_transposed(grad_values, value_ref[...])
+        grad_values = dot_plain(grad_proj, proj_turned[...]).astype(jnp.bfloat16)
+        grad_mod = dot_plain(grad_values, value_turned[...])
         normed = keep_norm[c]
 
         @pl.when(section > 0)
@@ -254,7 +325,14 @@
             inverse = keep_inv[c][:, 0:1]
             grad_in = grad_up + inverse * (grad_norm - centre_grad - normed * cross)
             g_out[c] = grad_in.astype(jnp.bfloat16)
+
+        @pl.when((section > 0) & ~hop_back)
+        def _():
             send_backward(c).start()
+
+        @pl.when(hop_back)
+        def _():
+            hop_backward(c).start()
 
         own_grad[0, at] = grad_values
         own_grad[1, at] = grad_proj
@@ -269,9 +347,9 @@
         table_sum[2] += folded(grad_up * keep_proj[c])
 
     def turn():
-        for kind, keep in ((0, keep_mod), (1, keep_val)):
+        for kind in range(2):
             for batch in range(batches):
-                part = keep[pl.ds(batch * per_micro, per_micro)].reshape(tok_micro, width)
+                part = pool[pl.ds(kind * tokens + batch * tok_micro, tok_micro)]
                 flipped = part.T.reshape(ys, zs, cores, tall, tok_micro)
                 for z in range(zs):
                     for to in range(cores):
@@ -280,11 +358,30 @@
                         ]
             share_turned(kind).start()
 
-    lag = LAG * (last - section)
+    def prepare():
+        tile = 256
+
+        @pl.loop(0, width // tile)
+        def _(j):
+            at = pl.ds(pl.multiple_of(j * tile, tile), tile)
+            value_turned[:, at] = value_ref[at, :].T
+            proj_turned[:, at] = proj_ref[at, :].T
+
+    load_value.wait()
+    load_proj.wait()
+    lag = jnp.where(relay_out, 2 * chunks, LAG * (last - section))
+    prepare_at = jnp.where((section == 0) & (lag >= chunks), chunks, 0)
     turn_at = jnp.where(lag >= chunks, chunks, chunks + lag)
 
-    @pl.loop(0, chunks + LAG * last + 1)
+    relay_from = jnp.where(relay_out, chunks, RELAY_LAG)
+    rounds = chunks + max(2 * chunks, LAG * last, RELAY_LAG) + 1
+
+    @pl.loop(0, rounds)
     def _(i):
+        @pl.when(i == prepare_at)
+        def _():
+            prepare()
+
         @pl.when(i < chunks)
         def _():
             forward(i)
@@ -292,6 +389,19 @@
         @pl.when(i == turn_at)
         def _():
             turn()
+
+        at = i - relay_from
+        within = (at >= 0) & (at < chunks)
+
+        @pl.when(within & relay_out)
+        def _():
+            hop_forward(at).wait_recv()
+            relay_forward(at).start()
+
+        @pl.when(within & relay_back)
+        def _():
+            hop_backward(at).wait_recv()
+            relay_backward(at).start()
 
         c = i - lag
 
@@ -355,9 +465,12 @@
             y_id(toward[kind]),
         )
 
+    def second_stage(seg, kind, way):
+        return pl.ds(((seg * 2 + kind) * 2 + way) * tall, tall)
+
     def second_move(seg, kind, way):
         return remote(
-            second_stage.at[seg, kind, way],
+            pool.at[second_stage(seg, kind, way)],
             second_got.at[seg, kind, way],
             second_send.at[seg, kind, way],
             second_recv.at[seg, kind, way],
@@ -379,25 +492,26 @@
             left = turned[kind, core, z_to].reshape(ys * tall, -1)
             left_peer = peer_turned[kind, z_to].reshape(ys * tall, -1)
             block = dot_plain(left, own_grad[kind]) + dot_plain(left_peer, peer_grad[kind])
-            own_sum[seg, kind] = block.reshape(ys, tall, width)
-            first_stage[seg, kind] = own_sum[seg, kind, across].astype(jnp.bfloat16)
+            fresh[...] = block.reshape(ys, tall, width)
+            first_stage[seg, kind] = fresh[across].astype(jnp.bfloat16)
             first_move(seg, kind).start()
+            onward, other = (ahead, behind) if kind == 0 else (behind, ahead)
+            pool[second_stage(seg, kind, 1 - kind)] = fresh[other].astype(jnp.bfloat16)
+            partial[seg, kind] = fresh[onward]
+            own_sum[seg, kind] = fresh[y_at]
 
     def second(seg):
         for kind in range(2):
-            for way, to in ((0, ahead), (1, behind)):
-                if way != kind:
-                    second_stage[seg, kind, way] = own_sum[seg, kind, to].astype(jnp.bfloat16)
-                    second_move(seg, kind, way).start()
-        for kind, to in ((0, ahead), (1, behind)):
+            second_move(seg, kind, 1 - kind).start()
+        for kind in range(2):
             first_move(seg, kind).wait_recv()
-            total = own_sum[seg, kind, to] + first_got[seg, kind].astype(jnp.float32)
-            second_stage[seg, kind, kind] = total.astype(jnp.bfloat16)
+            total = partial[seg, kind] + first_got[seg, kind].astype(jnp.float32)
+            pool[second_stage(seg, kind, kind)] = total.astype(jnp.bfloat16)
             second_move(seg, kind, kind).start()
 
     def third(seg):
         for kind in range(2):
-            total = own_sum[seg, kind, y_at]
+            total = own_sum[seg, kind]
             for way in range(2):
                 second_move(seg, kind, way).wait_recv()
                 total = total + second_got[seg, kind, way].astype(jnp.float32)
@@ -405,7 +519,7 @@
                 far_stage[seg, kind] = total.astype(jnp.bfloat16)
                 far_move(seg, kind).start()
             else:
-                own_sum[seg, kind, y_at] = total
+                own_sum[seg, kind] = total
 
     compute(0)
     for seg in range(zs):
@@ -427,7 +541,7 @@
         mine = mine + jnp.where(me == owner, table[:, owner * tall : (owner + 1) * tall], 0.0)
     table_out[...] = mine[:3]
     for kind, out in ((0, value_out), (1, proj_out)):
-        total = own_sum[zs - 1, kind, y_at]
+        total = own_sum[zs - 1, kind]
         for seg in range(zs - 1):
             far_move(seg, kind).wait_recv()
             total = total + far_got[seg, kind].astype(jnp.float32)
@@ -463,11 +577,30 @@
         def _():
             send_mirror(c).wait_send()
 
-
-def run_pipeline(mesh, inputs, out_grad, modulation, value_weight, proj_weight):
+        @pl.when(relay_out)
+        def _():
+            relay_forward(c).wait_send()
+
+        @pl.when(relay_back)
+        def _():
+            relay_backward(c).wait_send()
+
+
+def per_device(
+    mesh,
+    inputs,
+    out_grad,
+    guide_bin,
+    time_step,
+    guide_table,
+    section_table,
+    value_weight,
+    proj_weight,
+):
     batches, tok_dev, width = inputs.shape
-    value_width = value_weight.shape[1]
-    assert value_width == width
+    assert value_weight.shape[2] == width
+    assert guide_bin.shape[1] == 1
+    assert batches <= 8
     rows = min(ROWS, tok_dev)
     chunks = batches * tok_dev // rows
     tokens = batches * tok_dev
@@ -476,31 +609,39 @@
     tall = width // (ys * zs * cores)
     dims = (sections, ys, zs, cores, chunks, tok_dev // rows, rows)
     vmem = pl.BlockSpec(memory_space=pltpu.VMEM)
+    smem = pl.BlockSpec(memory_space=pltpu.SMEM)
     hbm = pl.BlockSpec(memory_space=pl.ANY)
     half, full = jnp.bfloat16, jnp.float32
 
     def sems(*shape):
         return pltpu.SemaphoreType.DMA(shape)
 
-    return pl.pallas_call(
+    block = pltpu.VMEM((chunks, rows, width), half)
+    wide = pltpu.VMEM((chunks, rows, width), full)
+    square = pltpu.VMEM((width, width), half)
+    value_part, proj_part, table_part = pl.pallas_call(
         functools.partial(pipeline_kernel, dims),
         out_shape=(
             jax.ShapeDtypeStruct((tall, width), full),
             jax.ShapeDtypeStruct((tall, width), full),
             jax.ShapeDtypeStruct((3, tall), full),
         ),
-        in_specs=[hbm, hbm, vmem, vmem, vmem],
+        in_specs=[hbm, hbm, smem, smem, vmem, vmem, hbm, hbm],
         out_specs=(vmem,) * 3,
         scratch_shapes=[
-            pltpu.VMEM((chunks, rows, width), half),
-            pltpu.VMEM((chunks, rows, width), half),
-            pltpu.VMEM((chunks, rows, width), half),
-            pltpu.VMEM((chunks, rows, width), half),
-            pltpu.VMEM((chunks, rows, width), half),
-            pltpu.VMEM((chunks, rows, width), half),
-            pltpu.VMEM((chunks, rows, width), full),
+            block,
+            block,
+            block,
+            block,
+            square,
+            square,
+            square,
+            square,
+            pltpu.VMEM((8, 3 * width), full),
+            pltpu.VMEM((max(2 * tokens, 4 * zs * tall), width), half),
+            wide,
             pltpu.VMEM((chunks, rows, 128), full),
-            pltpu.VMEM((chunks, rows, width), full),
+            wide,
             pltpu.VMEM((2, tokens, width), half),
             pltpu.VMEM((2, tokens, width), half),
             pltpu.VMEM((2, cores, zs, ys, tall, tokens), half),
@@ -511,10 +652,14 @@
             pltpu.VMEM((zs, 2, tall, width), half),
             pltpu.VMEM((zs, 2, tall, width), half),
             pltpu.VMEM((zs, 2, 2, tall, width), half),
-            pltpu.VMEM((zs, 2, 2, tall, width), half),
             pltpu.VMEM((zs - 1, 2, tall, width), half),
             pltpu.VMEM((zs - 1, 2, tall, width), half),
-            pltpu.VMEM((zs, 2, ys, tall, width), full),
+            pltpu.VMEM((ys, tall, width), full),
+            pltpu.VMEM((zs, 2, tall, width), full),
+            pltpu.VMEM((zs, 2, tall, width), full),
+            sems(chunks),
+            sems(2),
+            sems(chunks),
             sems(chunks),
             sems(chunks),
             sems(chunks),
@@ -540,31 +685,12 @@
     )(
         inputs.reshape(chunks, rows, width),
         out_grad.reshape(chunks, rows, width),
-        modulation,
-        value_weight,
-        proj_weight,
-    )
-
-
-def per_device(
-    mesh,
-    inputs,
-    out_grad,
-    guide_bin,
-    time_step,
-    guide_table,
-    section_table,
-    value_weight,
-    proj_weight,
-):
-    batches, tok_dev, width = inputs.shape
-    assert guide_bin.shape[1] == 1
-    condition = conditions(guide_bin, time_step, guide_table)
-    modulation = condition[:, 0] + section_table[0].reshape(-1)
-    modulation = modulation.reshape(batches, 3, width)
-    modulation = modulation + jnp.array([0.0, 1.0, 0.0], jnp.float32)[None, :, None]
-    value_part, proj_part, table_part = run_pipeline(
-        mesh, inputs, out_grad, modulation, value_weight[0], proj_weight[0]
+        guide_bin,
+        time_step,
+        guide_table,
+        section_table[0],
+        value_weight[0],
+        proj_weight[0],
     )
     return (value_part[None], proj_part[None], table_part[None])
 

time: 269 us -> 258 us (0.959); the launches traced: 269 us -> 255 us
  Pallas kernels: 260 us -> 246 us
  local copies, waits for them, and re-layouts: 5.37 us -> 8.59 us
    pallas_call x1, Pallas kernels: 260 us -> 246 us  [per_device(): pl.pallas_call(functools.partial(pipeline_kernel, dims), out_shape=(jax.S...]
    unnamed x6, local copies, waits for them, and re-layouts: 5.37 us -> 8.59 us
where the time goes in v3:
time: 258 us; the launch traced here: 255 us
  Pallas kernels  246 us (95%)
  local copies, waits for them, and re-layouts  8.59 us (3%)
    pallas_call x1, Pallas kernels, per_device(): pl.pallas_call(functools.partial(pipeline_kernel, dims), out_shape=(jax.S...  246 us
    unnamed x6, local copies, waits for them, and re-layouts  8.59 us

profile of v3, /device:TPU:1, one launch (start us, length us, event | category | flops | bytes accessed | tf_op | source)
XLA Modules:
  0.0 254.8 jit_solution(5632683979855594240)
XLA Ops:
  0.6 1.3 copy.11.bin_ref
  1.9 1.3 copy.12.step_ref
  3.3 1.3 copy.16
  4.6 245.6 %shard_map.103 = (f32[48,1536]{1,0:T(8,128)}, f32[48,1536]{1,0:T(8,128)}, f32[3,48]{1,0:T(4,128)}) custom-call(bf16[16,32,1536]{2,1,0:T(8,128)(2,1)} %bitcast.12, bf16[16,32,1536]{2,1,0:T(8,128)(2,1)} %bitcast.13, s32[4,1]{1,0:T(4,128)} %copy.11.bin_ref, s32[4,1]{1,0:T(4,128)} %copy.12.step_ref, bf16[32,4608]{1,0:T(8,128)(2,1)} %guide_ref.1, ...), custom_call_target="tpu_custom_call" | custom-call | tf_op jit(solution)/shard_map/pallas_call | solution.py:622
  250.2 1.2 copy.13
  251.4 1.7 copy.19
  253.1 1.7 copy.20

commit v4 on v3

--- a/solution.py
+++ b/solution.py
@@ -14,7 +14,7 @@
 NORM_FLOOR = 0.1
 ROWS = 32
 LAG = 3
-RELAY_LAG = 8
+CROSS_LAG = 2
 VMEM_LIMIT = 67043328
 MESH = pl.DeviceIdType.MESH
 
@@ -73,8 +73,6 @@
     bwd_send,
     bwd_recv,
     mirror_send,
-    relay_send,
-    relay_recv,
     grad_send,
     grad_recv,
     turn_send,
@@ -107,15 +105,6 @@
     prev_id = (jnp.maximum(section - 1, 0), y_at, prev_z, core)
     mirror_id = (section, y_at, mirrored, core)
     peer_id = (section, y_at, z_at, 1 - core)
-    inner = (z_at > 0) & (z_at < zs - 1)
-    hop_out = inner & (section == half - 1)
-    hop_back = inner & (section == half)
-    relay_out = inner & (section == 0)
-    relay_back = inner & (section == last)
-    first_id = (0, y_at, z_at, core)
-    last_id = (last, y_at, z_at, core)
-    cross_out = (half, y_at, mirrored, core)
-    cross_back = (half - 1, y_at, mirrored, core)
 
     def y_id(step):
         return (section, (y_at + step + ys) % ys, z_at, core)
@@ -142,18 +131,6 @@
     def send_backward(c):
         return remote(g_out.at[c], g_in.at[c], bwd_send.at[c], bwd_recv.at[c], prev_id)
 
-    def hop_forward(c):
-        return remote(x_out.at[c], g_out.at[c], fwd_send.at[c], relay_recv.at[c], first_id)
-
-    def hop_backward(c):
-        return remote(g_out.at[c], x_out.at[c], bwd_send.at[c], relay_recv.at[c], last_id)
-
-    def relay_forward(c):
-        return remote(g_out.at[c], x_in.at[c], relay_send.at[c], fwd_recv.at[c], cross_out)
-
-    def relay_backward(c):
-        return remote(x_out.at[c], g_in.at[c], relay_send.at[c], bwd_recv.at[c], cross_back)
-
     def send_mirror(c):
         return remote(out_grad_ref.at[c], g_in.at[c], mirror_send.at[c], bwd_recv.at[c], mirror_id)
 
@@ -204,27 +181,6 @@
     def _():
         greet(mirror_id)
 
-    @pl.when(relay_out)
-    def _():
-        greet((half - 1, y_at, z_at, core))
-        greet(cross_out)
-
-    @pl.when(hop_out)
-    def _():
-        greet(first_id)
-        greet((last, y_at, mirrored, core))
-
-    @pl.when(hop_back)
-    def _():
-        greet(last_id)
-        greet((0, y_at, mirrored, core))
-
-    @pl.when(relay_back)
-    def _():
-        greet((half, y_at, z_at, core))
-        greet(cross_back)
-
-    relays = relay_out | hop_out | hop_back | relay_back
     greet(peer_id)
     for step in range(1, ys):
         greet(y_id(step))
@@ -257,7 +213,7 @@
         whole = modulation_ref[pl.ds(batch, 1), :]
         return whole[:, :width], whole[:, width : 2 * width], whole[:, 2 * width :]
 
-    pl.semaphore_wait(barrier, jnp.where(section == 0, 1, 2) + jnp.where(relays, 2, 0) + ys + zs - 1)
+    pl.semaphore_wait(barrier, jnp.where(section == 0, 1, 2) + ys + zs - 1)
 
     @pl.when(section == last)
     def _():
@@ -291,14 +247,7 @@
         @pl.when(section < last)
         def _():
             x_out[c] = (hidden + gate * projected).astype(jnp.bfloat16)
-
-        @pl.when((section < last) & ~hop_out)
-        def _():
             send_forward(c).start()
-
-        @pl.when(hop_out)
-        def _():
-            hop_forward(c).start()
 
         pool[pl.ds(pl.multiple_of(c * rows, rows), rows)] = modulated
         pool[pl.ds(pl.multiple_of(tokens + c * rows, rows), rows)] = values
@@ -325,14 +274,7 @@
             inverse = keep_inv[c][:, 0:1]
             grad_in = grad_up + inverse * (grad_norm - centre_grad - normed * cross)
             g_out[c] = grad_in.astype(jnp.bfloat16)
-
-        @pl.when((section > 0) & ~hop_back)
-        def _():
             send_backward(c).start()
-
-        @pl.when(hop_back)
-        def _():
-            hop_backward(c).start()
 
         own_grad[0, at] = grad_values
         own_grad[1, at] = grad_proj
@@ -369,14 +311,11 @@
 
     load_value.wait()
     load_proj.wait()
-    lag = jnp.where(relay_out, 2 * chunks, LAG * (last - section))
+    lag = LAG * (last - section) + jnp.where(section < half, CROSS_LAG, 0)
     prepare_at = jnp.where((section == 0) & (lag >= chunks), chunks, 0)
     turn_at = jnp.where(lag >= chunks, chunks, chunks + lag)
 
-    relay_from = jnp.where(relay_out, chunks, RELAY_LAG)
-    rounds = chunks + max(2 * chunks, LAG * last, RELAY_LAG) + 1
-
-    @pl.loop(0, rounds)
+    @pl.loop(0, chunks + LAG * last + CROSS_LAG + 1)
     def _(i):
         @pl.when(i == prepare_at)
         def _():
@@ -389,19 +328,6 @@
         @pl.when(i == turn_at)
         def _():
             turn()
-
-        at = i - relay_from
-        within = (at >= 0) & (at < chunks)
-
-        @pl.when(within & relay_out)
-        def _():
-            hop_forward(at).wait_recv()
-            relay_forward(at).start()
-
-        @pl.when(within & relay_back)
-        def _():
-            hop_backward(at).wait_recv()
-            relay_backward(at).start()
 
         c = i - lag
 
@@ -576,14 +502,6 @@
         @pl.when(section == last)
         def _():
             send_mirror(c).wait_send()
-
-        @pl.when(relay_out)
-        def _():
-            relay_forward(c).wait_send()
-
-        @pl.when(relay_back)
-        def _():
-            relay_backward(c).wait_send()
 
 
 def per_device(
@@ -664,8 +582,6 @@
             sems(chunks),
             sems(chunks),
             sems(chunks),
-            sems(chunks),
-            sems(chunks),
             sems(2, chunks),
             sems(2, chunks),
             sems(2),

time: 258 us -> 248 us (0.961); the launches traced: 255 us -> 248 us
  Pallas kernels: 246 us -> 239 us
    pallas_call x1, Pallas kernels: 246 us -> 239 us  [per_device(): pl.pallas_call(functools.partial(pipeline_kernel, dims), out_shape=(jax.S...]
where the time goes in v4:
time: 248 us
  Pallas kernels  239 us (96%)
  local copies, waits for them, and re-layouts  8.59 us (3%)
    pallas_call x1, Pallas kernels, per_device(): pl.pallas_call(functools.partial(pipeline_kernel, dims), out_shape=(jax.S...  239 us
    unnamed x6, local copies, waits for them, and re-layouts  8.59 us

profile of v4, /device:TPU:1, one launch (start us, length us, event | category | flops | bytes accessed | tf_op | source)
XLA Modules:
  0.0 248.0 jit_solution(7150868549799550116)
XLA Ops:
  0.6 1.3 copy.11.bin_ref
  1.9 1.3 copy.12.step_ref
  3.3 1.3 copy.16
  4.6 238.7 %shard_map.103 = (f32[48,1536]{1,0:T(8,128)}, f32[48,1536]{1,0:T(8,128)}, f32[3,48]{1,0:T(4,128)}) custom-call(bf16[16,32,1536]{2,1,0:T(8,128)(2,1)} %bitcast.12, bf16[16,32,1536]{2,1,0:T(8,128)(2,1)} %bitcast.13, s32[4,1]{1,0:T(4,128)} %copy.11.bin_ref, s32[4,1]{1,0:T(4,128)} %copy.12.step_ref, bf16[32,4608]{1,0:T(8,128)(2,1)} %guide_ref.1, ...), custom_call_target="tpu_custom_call" | custom-call | tf_op jit(solution)/shard_map/pallas_call | solution.py:540
  243.3 1.2 copy.13
  244.6 1.7 copy.19
  246.3 1.7 copy.20

commit v5 on v3

--- a/solution.py
+++ b/solution.py
@@ -14,6 +14,7 @@
 NORM_FLOOR = 0.1
 ROWS = 32
 LAG = 3
+CROSS_LAG = 4
 RELAY_LAG = 8
 VMEM_LIMIT = 67043328
 MESH = pl.DeviceIdType.MESH
@@ -369,12 +370,13 @@
 
     load_value.wait()
     load_proj.wait()
-    lag = jnp.where(relay_out, 2 * chunks, LAG * (last - section))
+    lag = LAG * (last - section) + jnp.where(section < half, CROSS_LAG, 0)
+    lag = jnp.where(relay_out, 2 * chunks, lag)
     prepare_at = jnp.where((section == 0) & (lag >= chunks), chunks, 0)
     turn_at = jnp.where(lag >= chunks, chunks, chunks + lag)
 
     relay_from = jnp.where(relay_out, chunks, RELAY_LAG)
-    rounds = chunks + max(2 * chunks, LAG * last, RELAY_LAG) + 1
+    rounds = chunks + max(2 * chunks, LAG * last + CROSS_LAG, RELAY_LAG) + 1
 
     @pl.loop(0, rounds)
     def _(i):

time: 258 us -> 245 us (0.950)
  Pallas kernels: 246 us -> 233 us
    pallas_call x1, Pallas kernels: 246 us -> 233 us  [per_device(): pl.pallas_call(functools.partial(pipeline_kernel, dims), out_shape=(jax.S...]
where the time goes in v5:
time: 245 us; the launch traced here: 242 us
  Pallas kernels  233 us (95%)
  local copies, waits for them, and re-layouts  8.59 us (4%)
    pallas_call x1, Pallas kernels, per_device(): pl.pallas_call(functools.partial(pipeline_kernel, dims), out_shape=(jax.S...  233 us
    unnamed x6, local copies, waits for them, and re-layouts  8.59 us

profile of v5, /device:TPU:1, one launch (start us, length us, event | category | flops | bytes accessed | tf_op | source)
XLA Modules:
  0.0 242.0 jit_solution(14530412576140624970)
XLA Ops:
  0.6 1.3 copy.11.bin_ref
  1.9 1.3 copy.12.step_ref
  3.3 1.3 copy.16
  4.6 232.7 %shard_map.103 = (f32[48,1536]{1,0:T(8,128)}, f32[48,1536]{1,0:T(8,128)}, f32[3,48]{1,0:T(4,128)}) custom-call(bf16[16,32,1536]{2,1,0:T(8,128)(2,1)} %bitcast.12, bf16[16,32,1536]{2,1,0:T(8,128)(2,1)} %bitcast.13, s32[4,1]{1,0:T(4,128)} %copy.11.bin_ref, s32[4,1]{1,0:T(4,128)} %copy.12.step_ref, bf16[32,4608]{1,0:T(8,128)(2,1)} %guide_ref.1, ...), custom_call_target="tpu_custom_call" | custom-call | tf_op jit(solution)/shard_map/pallas_call | solution.py:624
  237.3 1.2 copy.13
  238.6 1.7 copy.19
  240.3 1.7 copy.20
